TPU v7x, 256 devices: a whole 4x4x8 slice. The times are simulated.
256 devices in a mesh: gx: 64 (over x, z_hi, y, core), gy: 4 (over z_lo).
Axes of the slice: x: 4, y: 4, z: 8 (z_hi: 2, z_lo: 4; z = z_hi * 4 + z_lo), core: 2. Of those that a mesh axis runs over, the one named last changes fastest.
Arguments:
- adjoint: float32 [9, 256, 128, 512], P(None, 'gx', 'gy'), may hold values from -6 to 6
- buoyancy: float32 [256, 128, 512], P('gx', 'gy'), may hold values from 0.5 to 2
- lame_lambda: float32 [256, 128, 512], P('gx', 'gy'), may hold values from 0.5 to 2
- shear_mu: float32 [256, 128, 512], P('gx', 'gy'), may hold values from 0.3 to 1.2
- packed: int32 [64, 64, 4, 12, 256], P('gx', None, 'gy'), may hold values from -2147483648 to 2147483646
- scales: float32 [64, 64, 4, 12], P('gx', None, 'gy'), may hold values from 0.005 to 0.05
- perm: int32 [64, 64], P('gx'), may hold values from 0 to 63, each once within a row
Outputs:
- adjoint_out: float32 [9, 256, 128, 512], P(None, 'gx', 'gy')
- gradients: float32 [2, 256, 128, 512], P(None, 'gx', 'gy')
Inputs may be any that keep to these rules, and one draw needn't show every extreme that they name: Each row of perm names every number 0 to 63 once. The words of packed are stored inputs and may cross devices as they are, four signed bytes to a word; only values that a program computes travel in float32.
All inputs are finite; a program needn't handle non-finite values.
Results may differ from a plain program's by a relative error of at most 0.0003.
Values sent between devices are 32-bit elements; how exact they have to be, the bound alone decides.
A program may use at most 128 MiB of HBM per device.

v0:
```python
import jax
import jax.numpy as jnp
from jax import lax
from jax.sharding import PartitionSpec as P

STEPS = 2


courant = 0.15


def passed_along(value, axis, steps):
    count = lax.axis_size(axis)
    first, last = (max(0, -steps), min(count, count - steps))
    return lax.ppermute(value, axis, [(source, source + steps) for source in range(first, last)])


def unpack(words):
    low = (words & 255) - 128
    middle = (jnp.right_shift(words, 8) & 255) - 128
    high = (jnp.right_shift(words, 16) & 255) - 128
    topmost = jnp.right_shift(words, 24)
    return jnp.concatenate([low, middle, high, topmost], axis=-1).astype(jnp.float32)


def inverse_order(row):
    count = row.shape[0]
    slots = jnp.arange(count, dtype=jnp.int32)
    hits = (row[None, :] == slots[:, None]).astype(jnp.int32)
    return jnp.sum(hits * slots[None, :], axis=1)


def frame(field, ahead_x, behind_x, ahead_y, behind_y):
    rows_x, rows_y, rows_z = field.shape
    zero_x = jnp.zeros((1, rows_y, rows_z), jnp.float32)
    lower_x = zero_x if behind_x is None else behind_x
    upper_x = zero_x if ahead_x is None else ahead_x
    middle = jnp.concatenate([lower_x, field, upper_x], axis=0)
    zero_y = jnp.zeros((rows_x, 1, rows_z), jnp.float32)
    lower_y = zero_y if behind_y is None else behind_y
    upper_y = zero_y if ahead_y is None else ahead_y
    lower_y = jnp.pad(lower_y, ((1, 1), (0, 0), (0, 0)))
    upper_y = jnp.pad(upper_y, ((1, 1), (0, 0), (0, 0)))
    joined = jnp.concatenate([lower_y, middle, upper_y], axis=1)
    return jnp.pad(joined, ((0, 0), (0, 0), (1, 1)))


def window(field, margin, out_margin, shift):
    start_x = margin - out_margin + shift[0]
    start_y = margin - out_margin + shift[1]
    start_z = 1 + shift[2]
    size_x = field.shape[0] - 2 * margin + 2 * out_margin
    size_y = field.shape[1] - 2 * margin + 2 * out_margin
    size_z = field.shape[2] - 2
    return lax.slice(
        field, (start_x, start_y, start_z), (start_x + size_x, start_y + size_y, start_z + size_z)
    )


def unit_shift(axis, amount):
    offsets = [0, 0, 0]
    offsets[axis] = amount
    return tuple(offsets)


def diff_ahead(field, axis, margin, out_margin):
    return window(field, margin, out_margin, unit_shift(axis, 1)) - window(
        field, margin, out_margin, (0, 0, 0)
    )


def diff_behind(field, axis, margin, out_margin):
    return window(field, margin, out_margin, (0, 0, 0)) - window(
        field, margin, out_margin, unit_shift(axis, -1)
    )


def move_velocity(velocity, stress, buoyancy, margin, out_margin):
    scaled = courant * buoyancy

    def ahead(field, axis):
        return diff_ahead(field, axis, margin, out_margin)

    def behind(field, axis):
        return diff_behind(field, axis, margin, out_margin)

    return [
        velocity[0] - scaled * (ahead(stress[0], 0) + behind(stress[3], 1) + behind(stress[4], 2)),
        velocity[1] - scaled * (behind(stress[3], 0) + ahead(stress[1], 1) + behind(stress[5], 2)),
        velocity[2] - scaled * (behind(stress[4], 0) + behind(stress[5], 1) + ahead(stress[2], 2)),
    ]


def strains(padded, margin):

    def ahead(field, axis):
        return diff_ahead(field, axis, margin, 0)

    def behind(field, axis):
        return diff_behind(field, axis, margin, 0)

    return [
        behind(padded[0], 0),
        behind(padded[1], 1),
        behind(padded[2], 2),
        ahead(padded[0], 1) + ahead(padded[1], 0),
        ahead(padded[0], 2) + ahead(padded[2], 0),
        ahead(padded[1], 2) + ahead(padded[2], 1),
    ]


def move_stress(stress, strain, lame_lambda, shear_mu):
    trace = strain[0] + strain[1] + strain[2]
    result = []
    for index in range(3):
        result.append(
            stress[index] - courant * (lame_lambda * trace + 2.0 * shear_mu * strain[index])
        )
    for index in range(3, 6):
        result.append(stress[index] - courant * shear_mu * strain[index])
    return result


def on_device(adjoint, buoyancy, lame_lambda, shear_mu, packed, scales, perm):
    cells_x, cells_y, cells_z = buoyancy.shape
    inverse = inverse_order(perm[0])
    words = lax.all_to_all(packed, "gx", split_axis=1, concat_axis=0, tiled=True)
    factor = lax.all_to_all(scales, "gx", split_axis=1, concat_axis=0, tiled=True)
    blocks = unpack(words[:, 0, 0]) * factor[:, 0, 0, :, None]
    ordered = jnp.take(blocks, inverse, axis=0)
    forward = jnp.transpose(ordered, (1, 0, 2)).reshape(blocks.shape[1], cells_x, cells_y, cells_z)
    velocity = [adjoint[index] for index in range(3)]
    stress = [adjoint[index] for index in range(3, 9)]
    grad_lambda = jnp.zeros(buoyancy.shape, jnp.float32)
    grad_mu = jnp.zeros(buoyancy.shape, jnp.float32)
    for step in range(STEPS):
        stress_xx, stress_yy, stress_zz, stress_xy, stress_xz, stress_yz = stress
        next_x = passed_along(stress_xx[0:1], "gx", -1)
        prior_x = passed_along(jnp.stack([stress_xy[-1:], stress_xz[-1:]]), "gx", 1)
        next_y = passed_along(stress_yy[:, 0:1], "gy", -1)
        prior_y = passed_along(jnp.stack([stress_xy[:, -1:], stress_yz[:, -1:]]), "gy", 1)
        framed = [
            frame(stress_xx, next_x, None, None, None),
            frame(stress_yy, None, None, next_y, None),
            frame(stress_zz, None, None, None, None),
            frame(stress_xy, None, prior_x[0], None, prior_y[0]),
            frame(stress_xz, None, prior_x[1], None, None),
            frame(stress_yz, None, None, None, prior_y[1]),
        ]
        velocity = move_velocity(velocity, framed, buoyancy, 1, 0)
        speed_x, speed_y, speed_z = velocity
        vel_next_x = passed_along(jnp.stack([speed_y[0:1], speed_z[0:1]]), "gx", -1)
        vel_prior_x = passed_along(speed_x[-1:], "gx", 1)
        vel_next_y = passed_along(jnp.stack([speed_x[:, 0:1], speed_z[:, 0:1]]), "gy", -1)
        vel_prior_y = passed_along(speed_y[:, -1:], "gy", 1)
        moved = [
            frame(speed_x, None, vel_prior_x, vel_next_y[0], None),
            frame(speed_y, vel_next_x[0], None, None, vel_prior_y),
            frame(speed_z, vel_next_x[1], None, vel_next_y[1], None),
        ]
        strain = strains(moved, 1)
        stress = move_stress(stress, strain, lame_lambda, shear_mu)
        trace = strain[0] + strain[1] + strain[2]
        stored = [forward[6 * step + index] for index in range(6)]
        grad_lambda = grad_lambda + trace * (stored[0] + stored[1] + stored[2])
        grad_mu = grad_mu + 2.0 * (
            strain[0] * stored[0] + strain[1] * stored[1] + strain[2] * stored[2]
        )
        grad_mu = grad_mu + strain[3] * stored[3] + strain[4] * stored[4] + strain[5] * stored[5]
    return (jnp.stack(velocity + stress), jnp.stack([grad_lambda, grad_mu]))


def solution(mesh):
    return jax.shard_map(
        on_device,
        mesh=mesh,
        in_specs=(
            P(None, "gx", "gy", None),
            P("gx", "gy", None),
            P("gx", "gy", None),
            P("gx", "gy", None),
            P("gx", None, "gy", None, None),
            P("gx", None, "gy", None),
            P("gx", None),
        ),
        out_specs=(P(None, "gx", "gy", None), P(None, "gx", "gy", None)),
        check_vma=False,
    )
```

profile of v0, /device:TPU:34, one launch (start us, length us, event | category | flops | bytes accessed | tf_op | source)
XLA Modules:
  0.0 200.9 jit_solution(1496756770010428238)
XLA Ops:
  0.6 14.1 %all-to-all-start = ((s32[1,64,1,12,256]{4,2,3,0,1:T(1,128)}), s32[1,64,1,12,256]{4,2,3,0,1:T(1,128)}, u32[]{:S(2)}, u32[]{:S(2)}) async-start(s32[1,64,1,12,256]{4,2,3,0,1:T(1,128)} %bitcast.137), calls=%async_computation | async-start | bytes 1572864 | tf_op jit(solution)/shard_map/all_to_all | solution.py:127
  14.7 1.5 slice_bitcast_fusion.20
  16.2 9.1 %collective-permute-start = (f32[1,32,512]{2,1,0:T(8,128)}, f32[1,32,512]{2,1,0:T(8,128)S(1)}, u32[]{:S(2)}, u32[]{:S(2)}) collective-permute-start(f32[1,32,512]{2,1,0:T(8,128)} %slice_bitcast_fusion.20), channel_id=1, source_target_pairs={{4,0},{8,4},{12,8},{16,12},{20,16},{24,20},{28,24},{32,28},{36,32}... | collective-permute-start | bytes 196616 | tf_op jit(solution)/shard_map/ppermute | solution.py:15
  25.3 1.6 stack.110
  26.9 2.2 %collective-permute-start.2 = (f32[2,1,32,512]{3,2,1,0:T(8,128)}, f32[2,1,32,512]{3,2,1,0:T(8,128)}, u32[]{:S(2)}, u32[]{:S(2)}) collective-permute-start(f32[2,1,32,512]{3,2,1,0:T(8,128)} %stack.110), channel_id=1, source_target_pairs={{0,4},{4,8},{8,12},{12,16},{16,20},{20,24},{24,28},{28,32},{32,36}... | collective-permute-start | bytes 393224 | tf_op jit(solution)/shard_map/ppermute | solution.py:15
  29.0 2.3 %slice_bitcast_fusion.1 = (f32[4,32,512]{2,1,0:T(8,128)S(1)}, f32[4,32,512]{2,1,0:T(8,128)S(1)}, f32[4,32,512]{2,1,0:T(8,128)S(1)}, f32[4,32,512]{2,1,0:T(8,128)...) fusion(f32[9,4,32,512]{3,2,1,0:T(8,128)} %param.7), kind=kLoop, calls=%fused_computation.226 | loop fusion | bytes 3145728 | tf_op jit(solution)/shard_map/squeeze | solution.py:133
  31.4 0.7 copy-done.42
  32.1 2.9 %collective-permute-start.4 = (f32[4,1,512]{2,1,0:T(1,128)S(1)}, f32[4,1,512]{2,1,0:T(1,128)S(1)}, u32[]{:S(2)}, u32[]{:S(2)}) collective-permute-start(f32[4,1,512]{2,1,0:T(1,128)S(1)} %slice.544), channel_id=1, source_target_pairs={{1,0},{2,1},{3,2},{5,4},{6,5},{7,6},{9,8},{10,9},{11,10},{13,12},{... | collective-permute-start | bytes 24584 | tf_op jit(solution)/shard_map/ppermute | solution.py:15
  35.0 2.9 %collective-permute-start.1 = (f32[2,4,1,512]{3,2,1,0:T(1,128)S(1)}, f32[2,4,1,512]{3,2,1,0:T(1,128)S(1)}, u32[]{:S(2)}, u32[]{:S(2)}) collective-permute-start(f32[2,4,1,512]{3,2,1,0:T(1,128)S(1)} %pad_maximum_fusion.68), channel_id=1, source_target_pairs={{0,1},{1,2},{2,3},{4,5},{5,6},{6,7},{8,9},{9,10},{10,11},{12,13},{... | collective-permute-start | bytes 49160 | tf_op jit(solution)/shard_map/ppermute | solution.py:15
  39.4 0.7 copy.49
  40.7 1.0 collective-permute-done.2
  41.7 0.9 slice_bitcast_fusion.19
  42.7 1.2 pad_maximum_fusion.6
  43.9 1.3 fusion.33
  45.5 1.3 fusion.27
  46.8 3.0 %collective-permute-start.5 = (f32[4,1,512]{2,1,0:T(1,128)S(1)}, f32[4,1,512]{2,1,0:T(1,128)S(1)}, u32[]{:S(2)}, u32[]{:S(2)}) collective-permute-start(f32[4,1,512]{2,1,0:T(1,128)S(1)} %slice.546), channel_id=1, source_target_pairs={{0,1},{1,2},{2,3},{4,5},{5,6},{6,7},{8,9},{9,10},{10,11},{12,13},{... | collective-permute-start | bytes 24584 | tf_op jit(solution)/shard_map/ppermute | solution.py:15
  49.9 2.8 %collective-permute-start.7 = (f32[2,4,1,512]{3,2,1,0:T(1,128)S(1)}, f32[2,4,1,512]{3,2,1,0:T(1,128)S(1)}, u32[]{:S(2)}, u32[]{:S(2)}) collective-permute-start(f32[2,4,1,512]{3,2,1,0:T(1,128)S(1)} %pad_maximum_fusion.69), channel_id=1, source_target_pairs={{1,0},{2,1},{3,2},{5,4},{6,5},{7,6},{9,8},{10,9},{11,10},{13,12},{... | collective-permute-start | bytes 49160 | tf_op jit(solution)/shard_map/ppermute | solution.py:15
  52.7 1.9 collective-permute-start.3
  54.6 10.6 %collective-permute-start.6 = (f32[2,1,32,512]{3,2,1,0:T(8,128)S(1)}, f32[2,1,32,512]{3,2,1,0:T(8,128)S(1)}, u32[]{:S(2)}, u32[]{:S(2)}) collective-permute-start(f32[2,1,32,512]{3,2,1,0:T(8,128)S(1)} %pad_maximum_fusion.65), channel_id=1, source_target_pairs={{4,0},{8,4},{12,8},{16,12},{20,16},{24,20},{28,24},{32,28},{36,32}... | collective-permute-start | bytes 393224 | tf_op jit(solution)/shard_map/ppermute | solution.py:15
  65.3 2.4 %collective-permute-done.6 = f32[2,1,32,512]{3,2,1,0:T(8,128)S(1)} collective-permute-done((f32[2,1,32,512]{3,2,1,0:T(8,128)S(1)}, f32[2,1,32,512]{3,2,1,0:T(8,128)S(1)}, u32[]{:S(2)}, u32[]{:S(2)}) %collective-permute-start.6) | collective-permute-done | bytes 131104 | tf_op jit(solution)/shard_map/ppermute | solution.py:15
  69.7 1.9 collective-permute-start.11
  71.6 12.1 %collective-permute-start.8 = (f32[1,32,512]{2,1,0:T(8,128)S(1)}, f32[1,32,512]{2,1,0:T(8,128)S(1)}, u32[]{:S(2)}, u32[]{:S(2)}) collective-permute-start(f32[1,32,512]{2,1,0:T(8,128)S(1)} %slice.554), channel_id=1, source_target_pairs={{4,0},{8,4},{12,8},{16,12},{20,16},{24,20},{28,24},{32,28},{36,32}... | collective-permute-start | bytes 196616 | tf_op jit(solution)/shard_map/ppermute | solution.py:15
  83.8 3.6 %collective-permute-start.9 = (f32[2,4,1,512]{3,2,1,0:T(1,128)S(1)}, f32[2,4,1,512]{3,2,1,0:T(1,128)S(1)}, u32[]{:S(2)}, u32[]{:S(2)}) collective-permute-start(f32[2,4,1,512]{3,2,1,0:T(1,128)S(1)} %pad_maximum_fusion.70), channel_id=1, source_target_pairs={{0,1},{1,2},{2,3},{4,5},{5,6},{6,7},{8,9},{9,10},{10,11},{12,13},{... | collective-permute-start | bytes 49160 | tf_op jit(solution)/shard_map/ppermute | solution.py:15
  87.4 1.9 collective-permute-start.10
  89.4 11.2 %collective-permute-done.10 = f32[2,1,32,512]{3,2,1,0:T(8,128)S(1)} collective-permute-done((f32[2,1,32,512]{3,2,1,0:T(8,128)S(1)}, f32[2,1,32,512]{3,2,1,0:T(8,128)S(1)}, u32[]{:S(2)}, u32[]{:S(2)}) %collective-permute-start.10) | collective-permute-done | bytes 131104 | tf_op jit(solution)/shard_map/ppermute | solution.py:15
  100.8 0.9 bitcast_dynamic-update-slice_fusion.8
  101.8 0.9 bitcast_dynamic-update-slice_fusion.7
  102.7 2.9 %collective-permute-start.13 = (f32[4,1,512]{2,1,0:T(1,128)S(1)}, f32[4,1,512]{2,1,0:T(1,128)S(1)}, u32[]{:S(2)}, u32[]{:S(2)}) collective-permute-start(f32[4,1,512]{2,1,0:T(1,128)S(1)} %slice.566), channel_id=1, source_target_pairs={{0,1},{1,2},{2,3},{4,5},{5,6},{6,7},{8,9},{9,10},{10,11},{12,13},{... | collective-permute-start | bytes 24584 | tf_op jit(solution)/shard_map/ppermute | solution.py:15
  105.7 0.9 bitcast_dynamic-update-slice_fusion.6
  106.6 2.9 %collective-permute-start.15 = (f32[2,4,1,512]{3,2,1,0:T(1,128)S(1)}, f32[2,4,1,512]{3,2,1,0:T(1,128)S(1)}, u32[]{:S(2)}, u32[]{:S(2)}) collective-permute-start(f32[2,4,1,512]{3,2,1,0:T(1,128)S(1)} %pad_maximum_fusion.71), channel_id=1, source_target_pairs={{1,0},{2,1},{3,2},{5,4},{6,5},{7,6},{9,8},{10,9},{11,10},{13,12},{... | collective-permute-start | bytes 49160 | tf_op jit(solution)/shard_map/ppermute | solution.py:15
  109.5 1.9 collective-permute-start.12
  111.5 10.6 %collective-permute-start.14 = (f32[2,1,32,512]{3,2,1,0:T(8,128)S(1)}, f32[2,1,32,512]{3,2,1,0:T(8,128)S(1)}, u32[]{:S(2)}, u32[]{:S(2)}) collective-permute-start(f32[2,1,32,512]{3,2,1,0:T(8,128)S(1)} %pad_maximum_fusion.67), channel_id=1, source_target_pairs={{4,0},{8,4},{12,8},{16,12},{20,16},{24,20},{28,24},{32,28},{36,32}... | collective-permute-start | bytes 393224 | tf_op jit(solution)/shard_map/ppermute | solution.py:15
  122.2 3.6 %collective-permute-done.14 = f32[2,1,32,512]{3,2,1,0:T(8,128)S(1)} collective-permute-done((f32[2,1,32,512]{3,2,1,0:T(8,128)S(1)}, f32[2,1,32,512]{3,2,1,0:T(8,128)S(1)}, u32[]{:S(2)}, u32[]{:S(2)}) %collective-permute-start.14) | collective-permute-done | bytes 131104 | tf_op jit(solution)/shard_map/ppermute | solution.py:15
  125.9 1.0 pad_maximum_fusion
  126.9 13.8 %all-to-all-start.1 = ((f32[1,64,1,12]{3,2,0,1:T(1,128)}), f32[1,64,1,12]{3,2,0,1:T(1,128)S(1)}, u32[]{:S(2)}, u32[]{:S(2)}) async-start(f32[1,64,1,12]{3,2,0,1:T(1,128)} %copy.49), calls=%async_computation.1 | async-start | bytes 65536 | tf_op jit(solution)/shard_map/all_to_all | solution.py:128
  140.7 3.0 %fusion.2 = (s32[64,12,256]{2,1,0:T(8,128)}, s32[64,12,256]{2,1,0:T(8,128)}, s32[64,12,256]{2,1,0:T(8,128)}) fusion(s32[1,64,1,12,256]{4,2,3,0,1:T(1,128)} %all-to-all-done), kind=kLoop, calls=%fused_computation.40 | loop fusion | flops 1572864 | bytes 3145728 | tf_op jit(solution)/shard_map/sub | solution.py:19
  143.7 1.3 fusion.9
  145.0 1.5 copy.48
  146.5 5.2 %all-to-all-done.1 = f32[1,64,1,12]{3,2,0,1:T(1,128)S(1)} async-done(((f32[1,64,1,12]{3,2,0,1:T(1,128)}), f32[1,64,1,12]{3,2,0,1:T(1,128)S(1)}, u32[]{:S(2)}, u32[]{:S(2)}) %all-to-all-start.1) | async-done | bytes 3104 | tf_op jit(solution)/shard_map/all_to_all | solution.py:128
  151.6 3.8 %fusion = f32[64,12,1024]{2,1,0:T(8,128)} fusion(s32[64,12,256]{2,1,0:T(8,128)} %copy.48, s32[64,12,256]{2,1,0:T(8,128)} %get-tuple-element.37, s32[64,12,256]{2,1,0:T(8,128)} %get-tuple-element.36, s32[64,12,256]{2,1,0:T(8,128)} %get-tuple-element.35, f32[64,12]{1,0:T(8,128)S(1)} %bitcast.138), kind=kLoop, calls=%fused_computation.2 | loop fusion | flops 3932160 | bytes 6294528 | tf_op jit(solution)/shard_map/mul | solution.py:129
  155.4 5.1 %gather_fusion = f32[64,12,1024]{2,1,0:T(8,128)} fusion(f32[64,12,1024]{2,1,0:T(8,128)} %fusion, s32[1024]{0:T(1024)} %pad_clamp_fusion), kind=kCustom, calls=%fused_computation | custom fusion | bytes 6291712 | tf_op jit(solution)/shard_map/jit(_take)/gather | solution.py:130
  160.5 2.5 %select_bitcast_fusion = f32[12,64,1024]{2,0,1:T(8,128)S(1)} fusion(f32[64,12,1024]{2,1,0:T(8,128)} %gather_fusion, pred[64]{0:T(512)(128)(4,1)S(1)} %copy-done.62), kind=kLoop, calls=%fused_computation.3 | loop fusion | flops 786432 | bytes 6291520 | tf_op jit(solution)/shard_map/jit(_take)/select_n | solution.py:130
  163.0 10.0 %slice_reduce_fusion.11 = (f32[64,1024]{1,0:T(8,128)}, f32[64,1024]{1,0:T(8,128)}, f32[64,1024]{1,0:T(8,128)}, f32[64,1024]{1,0:T(8,128)S(1)}, f32[64,1024]{1,0:...) fusion(f32[12,64,1024]{2,0,1:T(8,128)S(1)} %select_bitcast_fusion), kind=kLoop, calls=%fused_computation.171 | loop fusion | bytes 6291456 | tf_op jit(solution)/shard_map/slice | solution.py:164
  173.1 1.7 squeeze.137
  174.8 1.7 squeeze.142
  176.5 1.7 squeeze.141
  178.1 1.7 squeeze.140
  179.8 1.7 squeeze.139
  181.5 1.7 squeeze.138
  183.2 1.7 squeeze.148
  184.9 1.7 squeeze.147
  186.6 0.7 squeeze.146
  187.3 0.7 squeeze.145
  188.1 1.7 squeeze.144
  189.8 1.7 squeeze.143
  191.5 1.8 add_bitcast_fusion.1
  193.4 0.9 bitcast_dynamic-update-slice_fusion.5
  194.3 0.9 bitcast_dynamic-update-slice_fusion.4
  195.1 0.9 bitcast_dynamic-update-slice_fusion.3
  196.2 0.8 bitcast_dynamic-update-slice_fusion.2
  197.0 0.9 bitcast_dynamic-update-slice_fusion.1
  197.9 0.9 bitcast_dynamic-update-slice_fusion
  198.9 1.1 add_bitcast_fusion
  200.0 0.8 pad_maximum_fusion.48
  (197 shorter events, 4.8 us)
Async XLA Ops:
  0.6 37.4 %copy-start.63 = (s32[1,64]{1,0:T(1,128)S(1)}, s32[1,64]{1,0:T(1,128)}, u32[]{:S(2)}) copy-start(s32[1,64]{1,0:T(1,128)} %param.13) | copy-start | bytes 772
  0.6 38.7 %copy-start.61 = (f32[1,64,1,12]{1,2,3,0:T(1,128)S(1)}, f32[1,64,1,12]{1,2,3,0:T(1,128)}, u32[]{:S(2)}) copy-start(f32[1,64,1,12]{1,2,3,0:T(1,128)} %param.12) | copy-start | bytes 9220
  0.6 126.3 %all-to-all-start = ((s32[1,64,1,12,256]{4,2,3,0,1:T(1,128)}), s32[1,64,1,12,256]{4,2,3,0,1:T(1,128)}, u32[]{:S(2)}, u32[]{:S(2)}) async-start(s32[1,64,1,12,256]{4,2,3,0,1:T(1,128)} %bitcast.137), calls=%async_computation | async-start | bytes 1572864 | tf_op jit(solution)/shard_map/all_to_all | solution.py:127
  16.2 29.3 %collective-permute-start = (f32[1,32,512]{2,1,0:T(8,128)}, f32[1,32,512]{2,1,0:T(8,128)S(1)}, u32[]{:S(2)}, u32[]{:S(2)}) collective-permute-start(f32[1,32,512]{2,1,0:T(8,128)} %slice_bitcast_fusion.20), channel_id=1, source_target_pairs={{4,0},{8,4},{12,8},{16,12},{20,16},{24,20},{28,24},{32,28},{36,32}... | collective-permute-start | bytes 196616 | tf_op jit(solution)/shard_map/ppermute | solution.py:15
  26.9 17.0 %copy-start.1 = (f32[9,4,32,512]{3,2,1,0:T(8,128)S(1)}, f32[9,4,32,512]{3,2,1,0:T(8,128)}, u32[]{:S(2)}) copy-start(f32[9,4,32,512]{3,2,1,0:T(8,128)} %param.7) | copy-start | bytes 7077892
  26.9 17.0 %copy-start.2 = (f32[4,32,512]{2,1,0:T(8,128)S(1)}, f32[4,32,512]{2,1,0:T(8,128)}, u32[]{:S(2)}) copy-start(f32[4,32,512]{2,1,0:T(8,128)} %param.8) | copy-start | bytes 786436
  26.9 14.8 %collective-permute-start.2 = (f32[2,1,32,512]{3,2,1,0:T(8,128)}, f32[2,1,32,512]{3,2,1,0:T(8,128)}, u32[]{:S(2)}, u32[]{:S(2)}) collective-permute-start(f32[2,1,32,512]{3,2,1,0:T(8,128)} %stack.110), channel_id=1, source_target_pairs={{0,4},{4,8},{8,12},{12,16},{16,20},{20,24},{24,28},{28,32},{32,36}... | collective-permute-start | bytes 393224 | tf_op jit(solution)/shard_map/ppermute | solution.py:15
  31.4 12.5 %copy-start.27 = (f32[4,32,512]{2,1,0:T(8,128)}, f32[4,32,512]{2,1,0:T(8,128)S(1)}, u32[]{:S(2)}) copy-start(f32[4,32,512]{2,1,0:T(8,128)S(1)} %get-tuple-element.30) | copy-start | bytes 786436
  31.4 13.8 %copy-start.23 = (f32[4,32,512]{2,1,0:T(8,128)}, f32[4,32,512]{2,1,0:T(8,128)S(1)}, u32[]{:S(2)}) copy-start(f32[4,32,512]{2,1,0:T(8,128)S(1)} %get-tuple-element.32) | copy-start | bytes 786436
  32.1 13.1 %collective-permute-start.4 = (f32[4,1,512]{2,1,0:T(1,128)S(1)}, f32[4,1,512]{2,1,0:T(1,128)S(1)}, u32[]{:S(2)}, u32[]{:S(2)}) collective-permute-start(f32[4,1,512]{2,1,0:T(1,128)S(1)} %slice.544), channel_id=1, source_target_pairs={{1,0},{2,1},{3,2},{5,4},{6,5},{7,6},{9,8},{10,9},{11,10},{13,12},{... | collective-permute-start | bytes 24584 | tf_op jit(solution)/shard_map/ppermute | solution.py:15
  35.0 5.6 %collective-permute-start.1 = (f32[2,4,1,512]{3,2,1,0:T(1,128)S(1)}, f32[2,4,1,512]{3,2,1,0:T(1,128)S(1)}, u32[]{:S(2)}, u32[]{:S(2)}) collective-permute-start(f32[2,4,1,512]{3,2,1,0:T(1,128)S(1)} %pad_maximum_fusion.68), channel_id=1, source_target_pairs={{0,1},{1,2},{2,3},{4,5},{5,6},{6,7},{8,9},{9,10},{10,11},{12,13},{... | collective-permute-start | bytes 49160 | tf_op jit(solution)/shard_map/ppermute | solution.py:15
  45.5 22.5 %copy-start = (f32[4,32,512]{2,1,0:T(8,128)S(1)}, f32[4,32,512]{2,1,0:T(8,128)}, u32[]{:S(2)}) copy-start(f32[4,32,512]{2,1,0:T(8,128)} %param.10) | copy-start | bytes 786436
  45.5 22.5 %copy-start.8 = (f32[4,32,512]{2,1,0:T(8,128)S(1)}, f32[4,32,512]{2,1,0:T(8,128)}, u32[]{:S(2)}) copy-start(f32[4,32,512]{2,1,0:T(8,128)} %param.9) | copy-start | bytes 786436
  46.8 18.4 %collective-permute-start.5 = (f32[4,1,512]{2,1,0:T(1,128)S(1)}, f32[4,1,512]{2,1,0:T(1,128)S(1)}, u32[]{:S(2)}, u32[]{:S(2)}) collective-permute-start(f32[4,1,512]{2,1,0:T(1,128)S(1)} %slice.546), channel_id=1, source_target_pairs={{0,1},{1,2},{2,3},{4,5},{5,6},{6,7},{8,9},{9,10},{10,11},{12,13},{... | collective-permute-start | bytes 24584 | tf_op jit(solution)/shard_map/ppermute | solution.py:15
  49.9 15.4 %collective-permute-start.7 = (f32[2,4,1,512]{3,2,1,0:T(1,128)S(1)}, f32[2,4,1,512]{3,2,1,0:T(1,128)S(1)}, u32[]{:S(2)}, u32[]{:S(2)}) collective-permute-start(f32[2,4,1,512]{3,2,1,0:T(1,128)S(1)} %pad_maximum_fusion.69), channel_id=1, source_target_pairs={{1,0},{2,1},{3,2},{5,4},{6,5},{7,6},{9,8},{10,9},{11,10},{13,12},{... | collective-permute-start | bytes 49160 | tf_op jit(solution)/shard_map/ppermute | solution.py:15
  52.7 15.0 %collective-permute-start.3 = (f32[1,32,512]{2,1,0:T(8,128)S(1)}, f32[1,32,512]{2,1,0:T(8,128)S(1)}, u32[]{:S(2)}, u32[]{:S(2)}) collective-permute-start(f32[1,32,512]{2,1,0:T(8,128)S(1)} %slice.543), channel_id=1, source_target_pairs={{0,4},{4,8},{8,12},{12,16},{16,20},{20,24},{24,28},{28,32},{32,36}... | collective-permute-start | bytes 196616 | tf_op jit(solution)/shard_map/ppermute | solution.py:15
  54.6 13.1 %collective-permute-start.6 = (f32[2,1,32,512]{3,2,1,0:T(8,128)S(1)}, f32[2,1,32,512]{3,2,1,0:T(8,128)S(1)}, u32[]{:S(2)}, u32[]{:S(2)}) collective-permute-start(f32[2,1,32,512]{3,2,1,0:T(8,128)S(1)} %pad_maximum_fusion.65), channel_id=1, source_target_pairs={{4,0},{8,4},{12,8},{16,12},{20,16},{24,20},{28,24},{32,28},{36,32}... | collective-permute-start | bytes 393224 | tf_op jit(solution)/shard_map/ppermute | solution.py:15
  65.3 3.6 %copy-start.53 = (f32[6,1,512]{2,1,0:T(1,128)}, f32[6,1,512]{2,1,0:T(1,128)S(1)}, u32[]{:S(2)}) copy-start(f32[6,1,512]{2,1,0:T(1,128)S(1)} %pad.117) | copy-start | bytes 36868
  65.3 3.6 %copy-start.55 = (f32[6,1,512]{2,1,0:T(1,128)}, f32[6,1,512]{2,1,0:T(1,128)S(1)}, u32[]{:S(2)}) copy-start(f32[6,1,512]{2,1,0:T(1,128)S(1)} %pad.119) | copy-start | bytes 36868
  68.3 37.3 %copy-start.4 = (f32[4,32,512]{2,1,0:T(8,128)}, f32[4,32,512]{2,1,0:T(8,128)S(1)}, u32[]{:S(2)}) copy-start(f32[4,32,512]{2,1,0:T(8,128)S(1)} %get-tuple-element.26) | copy-start | bytes 786436
  68.3 37.3 %copy-start.19 = (f32[4,32,512]{2,1,0:T(8,128)}, f32[4,32,512]{2,1,0:T(8,128)S(1)}, u32[]{:S(2)}) copy-start(f32[4,32,512]{2,1,0:T(8,128)S(1)} %get-tuple-element.18) | copy-start | bytes 786436
  69.1 32.7 %copy-start.10 = (f32[4,32,512]{2,1,0:T(8,128)}, f32[4,32,512]{2,1,0:T(8,128)S(1)}, u32[]{:S(2)}) copy-start(f32[4,32,512]{2,1,0:T(8,128)S(1)} %get-tuple-element.28) | copy-start | bytes 786436
  69.1 36.5 %copy-start.6 = (f32[4,32,512]{2,1,0:T(8,128)}, f32[4,32,512]{2,1,0:T(8,128)S(1)}, u32[]{:S(2)}) copy-start(f32[4,32,512]{2,1,0:T(8,128)S(1)} %get-tuple-element.27) | copy-start | bytes 786436
  69.7 32.1 %copy-start.21 = (f32[4,32,512]{2,1,0:T(8,128)}, f32[4,32,512]{2,1,0:T(8,128)S(1)}, u32[]{:S(2)}) copy-start(f32[4,32,512]{2,1,0:T(8,128)S(1)} %get-tuple-element.25) | copy-start | bytes 786436
  69.7 32.1 %copy-start.24 = (f32[4,32,512]{2,1,0:T(8,128)}, f32[4,32,512]{2,1,0:T(8,128)S(1)}, u32[]{:S(2)}) copy-start(f32[4,32,512]{2,1,0:T(8,128)S(1)} %get-tuple-element.24) | copy-start | bytes 786436
  69.7 32.1 %collective-permute-start.11 = (f32[4,1,512]{2,1,0:T(1,128)S(1)}, f32[4,1,512]{2,1,0:T(1,128)S(1)}, u32[]{:S(2)}, u32[]{:S(2)}) collective-permute-start(f32[4,1,512]{2,1,0:T(1,128)S(1)} %slice.563), channel_id=1, source_target_pairs={{1,0},{2,1},{3,2},{5,4},{6,5},{7,6},{9,8},{10,9},{11,10},{13,12},{... | collective-permute-start | bytes 24584 | tf_op jit(solution)/shard_map/ppermute | solution.py:15
  71.6 29.2 %collective-permute-start.8 = (f32[1,32,512]{2,1,0:T(8,128)S(1)}, f32[1,32,512]{2,1,0:T(8,128)S(1)}, u32[]{:S(2)}, u32[]{:S(2)}) collective-permute-start(f32[1,32,512]{2,1,0:T(8,128)S(1)} %slice.554), channel_id=1, source_target_pairs={{4,0},{8,4},{12,8},{16,12},{20,16},{24,20},{28,24},{32,28},{36,32}... | collective-permute-start | bytes 196616 | tf_op jit(solution)/shard_map/ppermute | solution.py:15
  83.8 5.6 %collective-permute-start.9 = (f32[2,4,1,512]{3,2,1,0:T(1,128)S(1)}, f32[2,4,1,512]{3,2,1,0:T(1,128)S(1)}, u32[]{:S(2)}, u32[]{:S(2)}) collective-permute-start(f32[2,4,1,512]{3,2,1,0:T(1,128)S(1)} %pad_maximum_fusion.70), channel_id=1, source_target_pairs={{0,1},{1,2},{2,3},{4,5},{5,6},{6,7},{8,9},{9,10},{10,11},{12,13},{... | collective-permute-start | bytes 49160 | tf_op jit(solution)/shard_map/ppermute | solution.py:15
  87.4 13.2 %collective-permute-start.10 = (f32[2,1,32,512]{3,2,1,0:T(8,128)S(1)}, f32[2,1,32,512]{3,2,1,0:T(8,128)S(1)}, u32[]{:S(2)}, u32[]{:S(2)}) collective-permute-start(f32[2,1,32,512]{3,2,1,0:T(8,128)S(1)} %pad_maximum_fusion.66), channel_id=1, source_target_pairs={{0,4},{4,8},{8,12},{12,16},{16,20},{20,24},{24,28},{28,32},{32,36}... | collective-permute-start | bytes 393224 | tf_op jit(solution)/shard_map/ppermute | solution.py:15
  102.7 19.3 %collective-permute-start.13 = (f32[4,1,512]{2,1,0:T(1,128)S(1)}, f32[4,1,512]{2,1,0:T(1,128)S(1)}, u32[]{:S(2)}, u32[]{:S(2)}) collective-permute-start(f32[4,1,512]{2,1,0:T(1,128)S(1)} %slice.566), channel_id=1, source_target_pairs={{0,1},{1,2},{2,3},{4,5},{5,6},{6,7},{8,9},{9,10},{10,11},{12,13},{... | collective-permute-start | bytes 24584 | tf_op jit(solution)/shard_map/ppermute | solution.py:15
  106.6 15.5 %collective-permute-start.15 = (f32[2,4,1,512]{3,2,1,0:T(1,128)S(1)}, f32[2,4,1,512]{3,2,1,0:T(1,128)S(1)}, u32[]{:S(2)}, u32[]{:S(2)}) collective-permute-start(f32[2,4,1,512]{3,2,1,0:T(1,128)S(1)} %pad_maximum_fusion.71), channel_id=1, source_target_pairs={{1,0},{2,1},{3,2},{5,4},{6,5},{7,6},{9,8},{10,9},{11,10},{13,12},{... | collective-permute-start | bytes 49160 | tf_op jit(solution)/shard_map/ppermute | solution.py:15
  109.5 16.3 %collective-permute-start.12 = (f32[1,32,512]{2,1,0:T(8,128)S(1)}, f32[1,32,512]{2,1,0:T(8,128)S(1)}, u32[]{:S(2)}, u32[]{:S(2)}) collective-permute-start(f32[1,32,512]{2,1,0:T(8,128)S(1)} %slice.565), channel_id=1, source_target_pairs={{0,4},{4,8},{8,12},{12,16},{16,20},{20,24},{24,28},{28,32},{32,36}... | collective-permute-start | bytes 196616 | tf_op jit(solution)/shard_map/ppermute | solution.py:15
  111.5 14.3 %collective-permute-start.14 = (f32[2,1,32,512]{3,2,1,0:T(8,128)S(1)}, f32[2,1,32,512]{3,2,1,0:T(8,128)S(1)}, u32[]{:S(2)}, u32[]{:S(2)}) collective-permute-start(f32[2,1,32,512]{3,2,1,0:T(8,128)S(1)} %pad_maximum_fusion.67), channel_id=1, source_target_pairs={{4,0},{8,4},{12,8},{16,12},{20,16},{24,20},{28,24},{32,28},{36,32}... | collective-permute-start | bytes 393224 | tf_op jit(solution)/shard_map/ppermute | solution.py:15
  122.1 21.6 %copy-start.51 = (f32[6,1,512]{2,1,0:T(1,128)}, f32[6,1,512]{2,1,0:T(1,128)S(1)}, u32[]{:S(2)}) copy-start(f32[6,1,512]{2,1,0:T(1,128)S(1)} %pad.128) | copy-start | bytes 36868
  122.1 21.5 %copy-start.57 = (f32[6,1,512]{2,1,0:T(1,128)}, f32[6,1,512]{2,1,0:T(1,128)S(1)}, u32[]{:S(2)}) copy-start(f32[6,1,512]{2,1,0:T(1,128)S(1)} %pad.131) | copy-start | bytes 36868
  122.2 21.5 %copy-start.59 = (f32[6,1,512]{2,1,0:T(1,128)}, f32[6,1,512]{2,1,0:T(1,128)S(1)}, u32[]{:S(2)}) copy-start(f32[6,1,512]{2,1,0:T(1,128)S(1)} %pad.129) | copy-start | bytes 36868
  125.8 17.8 %copy-start.40 = (f32[1,32,512]{2,1,0:T(8,128)}, f32[1,32,512]{2,1,0:T(8,128)S(1)}, u32[]{:S(2)}) copy-start(f32[1,32,512]{2,1,0:T(8,128)S(1)} %get-tuple-element.39) | copy-start | bytes 196612
  125.8 17.8 %copy-start.34 = (f32[1,32,512]{2,1,0:T(8,128)}, f32[1,32,512]{2,1,0:T(8,128)S(1)}, u32[]{:S(2)}) copy-start(f32[1,32,512]{2,1,0:T(8,128)S(1)} %collective-permute-done.12) | copy-start | bytes 196612
  126.9 24.7 %all-to-all-start.1 = ((f32[1,64,1,12]{3,2,0,1:T(1,128)}), f32[1,64,1,12]{3,2,0,1:T(1,128)S(1)}, u32[]{:S(2)}, u32[]{:S(2)}) async-start(f32[1,64,1,12]{3,2,0,1:T(1,128)} %copy.49), calls=%async_computation.1 | async-start | bytes 65536 | tf_op jit(solution)/shard_map/all_to_all | solution.py:128
  155.4 5.1 %copy-start.62 = (pred[64]{0:T(512)(128)(4,1)S(1)}, pred[64]{0:T(512)(128)(4,1)}, u32[]{:S(2)}) copy-start(pred[64]{0:T(512)(128)(4,1)} %compare_and_fusion) | copy-start | bytes 196
  188.1 5.3 %copy-start.9 = (f32[4,32,512]{2,1,0:T(8,128)S(1)}, f32[4,32,512]{2,1,0:T(8,128)}, u32[]{:S(2)}) copy-start(f32[4,32,512]{2,1,0:T(8,128)} %param.9) | copy-start | bytes 786436
  188.1 5.3 %copy-start.22 = (f32[4,32,512]{2,1,0:T(8,128)S(1)}, f32[4,32,512]{2,1,0:T(8,128)}, u32[]{:S(2)}) copy-start(f32[4,32,512]{2,1,0:T(8,128)} %copy-done.21) | copy-start | bytes 786436
  191.5 2.8 %copy-start.25 = (f32[4,32,512]{2,1,0:T(8,128)S(1)}, f32[4,32,512]{2,1,0:T(8,128)}, u32[]{:S(2)}) copy-start(f32[4,32,512]{2,1,0:T(8,128)} %copy-done.24) | copy-start | bytes 786436
  191.5 2.8 %copy-start.52 = (f32[6,1,512]{2,1,0:T(1,128)S(1)}, f32[6,1,512]{2,1,0:T(1,128)}, u32[]{:S(2)}) copy-start(f32[6,1,512]{2,1,0:T(1,128)} %copy-done.51) | copy-start | bytes 36868
  194.2 2.8 %copy-start.5 = (f32[4,32,512]{2,1,0:T(8,128)S(1)}, f32[4,32,512]{2,1,0:T(8,128)}, u32[]{:S(2)}) copy-start(f32[4,32,512]{2,1,0:T(8,128)} %copy-done.4) | copy-start | bytes 786436
  194.2 2.8 %copy-start.41 = (f32[1,32,512]{2,1,0:T(8,128)S(1)}, f32[1,32,512]{2,1,0:T(8,128)}, u32[]{:S(2)}) copy-start(f32[1,32,512]{2,1,0:T(8,128)} %copy-done.40) | copy-start | bytes 196612
  195.1 2.8 %copy-start.7 = (f32[4,32,512]{2,1,0:T(8,128)S(1)}, f32[4,32,512]{2,1,0:T(8,128)}, u32[]{:S(2)}) copy-start(f32[4,32,512]{2,1,0:T(8,128)} %copy-done.6) | copy-start | bytes 786436
  195.1 2.8 %copy-start.12 = (f32[6,34,512]{2,1,0:T(8,128)S(1)}, f32[6,34,512]{2,1,0:T(8,128)}, u32[]{:S(2)}) copy-start(f32[6,34,512]{2,1,0:T(8,128)} %get-tuple-element.46) | copy-start | bytes 1253380
  195.1 2.8 %copy-start.60 = (f32[6,1,512]{2,1,0:T(1,128)S(1)}, f32[6,1,512]{2,1,0:T(1,128)}, u32[]{:S(2)}) copy-start(f32[6,1,512]{2,1,0:T(1,128)} %copy-done.59) | copy-start | bytes 36868
  196.0 2.7 %copy-start.14 = (f32[6,34,512]{2,1,0:T(8,128)S(1)}, f32[6,34,512]{2,1,0:T(8,128)}, u32[]{:S(2)}) copy-start(f32[6,34,512]{2,1,0:T(8,128)} %copy-done.13) | copy-start | bytes 1253380
  196.0 2.7 %copy-start.16 = (f32[6,34,512]{2,1,0:T(8,128)S(1)}, f32[6,34,512]{2,1,0:T(8,128)}, u32[]{:S(2)}) copy-start(f32[6,34,512]{2,1,0:T(8,128)} %copy-done.15) | copy-start | bytes 1253380
  196.0 2.7 %copy-start.18 = (f32[6,34,512]{2,1,0:T(8,128)S(1)}, f32[6,34,512]{2,1,0:T(8,128)}, u32[]{:S(2)}) copy-start(f32[6,34,512]{2,1,0:T(8,128)} %copy-done.17) | copy-start | bytes 1253380
  196.0 2.7 %copy-start.28 = (f32[4,32,512]{2,1,0:T(8,128)S(1)}, f32[4,32,512]{2,1,0:T(8,128)}, u32[]{:S(2)}) copy-start(f32[4,32,512]{2,1,0:T(8,128)} %squeeze.137) | copy-start | bytes 786436
  196.1 2.7 %copy-start.29 = (f32[4,32,512]{2,1,0:T(8,128)S(1)}, f32[4,32,512]{2,1,0:T(8,128)}, u32[]{:S(2)}) copy-start(f32[4,32,512]{2,1,0:T(8,128)} %squeeze.142) | copy-start | bytes 786436
  196.1 2.7 %copy-start.30 = (f32[4,32,512]{2,1,0:T(8,128)S(1)}, f32[4,32,512]{2,1,0:T(8,128)}, u32[]{:S(2)}) copy-start(f32[4,32,512]{2,1,0:T(8,128)} %squeeze.141) | copy-start | bytes 786436
  196.1 2.7 %copy-start.31 = (f32[4,32,512]{2,1,0:T(8,128)S(1)}, f32[4,32,512]{2,1,0:T(8,128)}, u32[]{:S(2)}) copy-start(f32[4,32,512]{2,1,0:T(8,128)} %squeeze.140) | copy-start | bytes 786436
  196.1 2.7 %copy-start.32 = (f32[4,32,512]{2,1,0:T(8,128)S(1)}, f32[4,32,512]{2,1,0:T(8,128)}, u32[]{:S(2)}) copy-start(f32[4,32,512]{2,1,0:T(8,128)} %squeeze.139) | copy-start | bytes 786436
  196.1 2.7 %copy-start.33 = (f32[4,32,512]{2,1,0:T(8,128)S(1)}, f32[4,32,512]{2,1,0:T(8,128)}, u32[]{:S(2)}) copy-start(f32[4,32,512]{2,1,0:T(8,128)} %squeeze.138) | copy-start | bytes 786436
  196.1 2.7 %copy-start.37 = (f32[1,32,512]{2,1,0:T(8,128)S(1)}, f32[1,32,512]{2,1,0:T(8,128)}, u32[]{:S(2)}) copy-start(f32[1,32,512]{2,1,0:T(8,128)} %copy-done.36) | copy-start | bytes 196612
  196.1 2.7 %copy-start.39 = (f32[1,32,512]{2,1,0:T(8,128)S(1)}, f32[1,32,512]{2,1,0:T(8,128)}, u32[]{:S(2)}) copy-start(f32[1,32,512]{2,1,0:T(8,128)} %copy-done.38) | copy-start | bytes 196612
  196.1 2.7 %copy-start.45 = (f32[4,32,512]{2,1,0:T(8,128)S(1)}, f32[4,32,512]{2,1,0:T(8,128)}, u32[]{:S(2)}) copy-start(f32[4,32,512]{2,1,0:T(8,128)} %squeeze.148) | copy-start | bytes 786436
  196.1 2.7 %copy-start.46 = (f32[4,32,512]{2,1,0:T(8,128)S(1)}, f32[4,32,512]{2,1,0:T(8,128)}, u32[]{:S(2)}) copy-start(f32[4,32,512]{2,1,0:T(8,128)} %squeeze.147) | copy-start | bytes 786436
  196.1 2.7 %copy-start.47 = (f32[4,32,512]{2,1,0:T(8,128)S(1)}, f32[4,32,512]{2,1,0:T(8,128)}, u32[]{:S(2)}) copy-start(f32[4,32,512]{2,1,0:T(8,128)} %squeeze.146) | copy-start | bytes 786436
  196.2 2.7 %copy-start.48 = (f32[4,32,512]{2,1,0:T(8,128)S(1)}, f32[4,32,512]{2,1,0:T(8,128)}, u32[]{:S(2)}) copy-start(f32[4,32,512]{2,1,0:T(8,128)} %squeeze.145) | copy-start | bytes 786436
  (18 other events, 32.3 us)
where the time goes:
time: 203 us; the launch traced here: 201 us
  starting transfers between devices  101 us (50%)
  local copies, waits for them, and re-layouts  44 us (22%)
  other arithmetic  29.7 us (15%)
  waiting for transfers between devices  24.1 us (12%)
    ppermute x16, starting transfers between devices, passed_along(): lax.ppermute(value, axis, [(source, source + steps) for source in range(f...  73.3 us
    ppermute x16, waiting for transfers between devices, passed_along(): lax.ppermute(value, axis, [(source, source + steps) for source in range(f...  18.9 us
    squeeze x12, local copies, waits for them, and re-layouts, on_device(): stored = [forward[6 * step + index] for index in range(6)]  18.4 us
    all_to_all x1, starting transfers between devices, on_device(): lax.all_to_all(packed, 'gx', split_axis=1, concat_axis=0, tiled=True)  14.1 us
    all_to_all x1, starting transfers between devices, on_device(): lax.all_to_all(scales, 'gx', split_axis=1, concat_axis=0, tiled=True)  13.8 us
    slice x1, local copies, waits for them, and re-layouts, on_device(): stored = [forward[6 * step + index] for index in range(6)]  10 us
    unnamed x8, other arithmetic  7 us
    all_to_all x1, waiting for transfers between devices, on_device(): lax.all_to_all(scales, 'gx', split_axis=1, concat_axis=0, tiled=True)  5.15 us
  transfers between devices with their start and end apart: 18, of which 6 were waited for; matrix products, arithmetic and copies ran while one was open for 12% of the time, Pallas kernels for 0%

commit v1 on v0

v1 whole, which is shorter than its diff:
```python
import functools

import jax
import jax.numpy as jnp
from jax import lax
from jax.experimental import pallas as pl
from jax.experimental.pallas import tpu as pltpu
from jax.sharding import PartitionSpec as P

MESH = pl.DeviceIdType.MESH
COURANT = 0.15
VX, VY, VZ, SXX, SYY, SZZ, SXY, SXZ, SYZ = range(9)
NX, NY, NZ = 4, 32, 512
TOP, END = 8, 40
LAST = NX
SCALE_UNIT = 2.0**31


def inverse_order(row):
    count = row.shape[0]
    slots = jnp.arange(count, dtype=jnp.int32)
    hits = (row[None, :] == slots[:, None]).astype(jnp.int32)
    return jnp.sum(hits * slots[None, :], axis=1)


def rows_of(shape):
    return lax.broadcasted_iota(jnp.int32, shape, 0)


def lanes_of(shape):
    return lax.broadcasted_iota(jnp.int32, shape, 1)


def z_ahead(x):
    return jnp.where(lanes_of(x.shape) == NZ - 1, 0.0, pltpu.roll(x, NZ - 1, 1))


def z_behind(x):
    return jnp.where(lanes_of(x.shape) == 0, 0.0, pltpu.roll(x, 1, 1))


def y_ahead(x, following):
    return pltpu.roll(jnp.where(rows_of(x.shape) == 0, following, x), 7, 0)


def y_behind(x, preceding):
    return pltpu.roll(jnp.where(rows_of(x.shape) == 7, preceding, x), 1, 0)


def kernel(
    count, rows_gy,
    adjoint, buoyancy, lame, shear, words, factors, inverse,
    out, gradients,
    field, mat_b, mat_l, mat_m, strain, grad, held, landed,
    to_lo, to_hi, to_south, to_north, to_corner,
    from_lo, from_hi, from_south, from_north, from_corner,
    load_sem, send_sem, recv_sem, halo_send, halo_recv, out_sem,
):
    me, row = lax.axis_index("gx"), lax.axis_index("gy")
    own_x, own_y = pl.ds(1, NX), pl.ds(TOP, NY)
    has_lo, has_hi = me > 0, me < count - 1
    has_south, has_north = row > 0, row < rows_gy - 1

    loads = [
        pltpu.make_async_copy(adjoint, field.at[:, own_x, own_y, :], load_sem.at[0]),
        pltpu.make_async_copy(buoyancy, mat_b, load_sem.at[1]),
        pltpu.make_async_copy(words, held.at[:, pl.ds(0, 24), :], load_sem.at[2]),
        pltpu.make_async_copy(factors, held.at[:, pl.ds(24, 1), :], load_sem.at[3]),
        pltpu.make_async_copy(lame, mat_l, load_sem.at[4]),
        pltpu.make_async_copy(shear, mat_m, load_sem.at[5]),
    ]
    for load in loads:
        load.start()

    def exchange_peer(t):
        far = 1 - t % 2
        u = t // 2 + (1 - far)
        x, z, y, core = me // 16, (me // 8) % 2, (me // 2) % 4, me % 2
        return (
            ((x + u // 8) % 4) * 16 + ((z + far) % 2) * 8 + ((y + (u // 2) % 4) % 4) * 2 + (core + u % 2) % 2
        )

    exists = {
        (-1, 0): has_lo, (1, 0): has_hi, (0, -1): has_south, (0, 1): has_north,
        (-1, -1): has_lo & has_south, (1, 1): has_hi & has_north,
        (1, -1): has_hi & has_south, (-1, 1): has_lo & has_north,
    }

    barrier = pltpu.get_barrier_semaphore()

    def greet(t, _):
        pl.semaphore_signal(barrier, inc=1, device_id={"gx": exchange_peer(t)}, device_id_type=MESH)
        return 0

    lax.fori_loop(0, count - 1, greet, 0)
    expected = jnp.int32(count - 1)
    for (dx, dy), there in exists.items():
        if dy != 0:
            expected = expected + there.astype(jnp.int32)

            @pl.when(there)
            def _():
                pl.semaphore_signal(
                    barrier, inc=1, device_id={"gx": me + dx, "gy": row + dy}, device_id_type=MESH
                )

    for there, ref in ((has_lo, from_lo), (has_hi, from_hi), (has_south, from_south), (has_north, from_north)):

        @pl.when(jnp.logical_not(there))
        def _():
            ref[...] = jnp.zeros(ref.shape, jnp.float32)

    corners = ((-1, -1), (1, 1), (1, -1), (-1, 1))
    for slot, where in enumerate(corners):

        @pl.when(jnp.logical_not(exists[where]))
        def _():
            for step in range(2):
                from_corner[step, slot] = jnp.zeros((2, NZ), jnp.float32)

    def tile(f, layer, k):
        return field[f, layer, pl.ds(TOP + 8 * k, 8), :]

    nothing = jnp.zeros((8, NZ), jnp.float32)

    def stage(step):
        for k in range(NY // 8):
            at = pl.ds(8 * k, 8)
            b = COURANT * mat_b[0, at, :]
            sxy, sxz, syy, syz, szz = (tile(f, 1, k) for f in (SXY, SXZ, SYY, SYZ, SZZ))
            syy_next = tile(SYY, 1, k + 1) if k < NY // 8 - 1 else nothing
            syz_prior = tile(SYZ, 1, k - 1) if k > 0 else nothing
            to_lo[step, 0, at, :] = tile(VY, 1, k) - b * (sxy + y_ahead(syy, syy_next) - syy + syz - z_behind(syz))
            to_lo[step, 1, at, :] = tile(VZ, 1, k) - b * (
                sxz + syz - y_behind(syz, syz_prior) + z_ahead(szz) - szz
            )
            to_lo[step, 2, at, :] = tile(SXX, 1, k)
            b = COURANT * mat_b[NX - 1, at, :]
            sxx, sxy, sxz = (tile(f, LAST, k) for f in (SXX, SXY, SXZ))
            sxy_prior = tile(SXY, LAST, k - 1) if k > 0 else nothing
            to_hi[step, 0, at, :] = tile(VX, LAST, k) - b * (
                sxy - y_behind(sxy, sxy_prior) - sxx + sxz - z_behind(sxz)
            )
            to_hi[step, 1, at, :] = sxy
            to_hi[step, 2, at, :] = sxz
            if step == 0:
                to_lo[0, 3, at, :] = mat_b[0, at, :]
                to_hi[0, 3, at, :] = mat_b[NX - 1, at, :]
        for i in range(NX):
            layer, at = i + 1, pl.ds(0, 8)
            raw = mat_b[i, at, :]
            b = COURANT * raw
            sxx, sxy, sxz, syy, syz, szz = (tile(f, layer, 0) for f in (SXX, SXY, SXZ, SYY, SYZ, SZZ))
            sxx_next = tile(SXX, layer + 1, 0) if i < NX - 1 else nothing
            sxz_prior = tile(SXZ, layer - 1, 0) if i > 0 else nothing
            rx = tile(VX, layer, 0) - b * (sxx_next - sxx + sxy + sxz - z_behind(sxz))
            rz = tile(VZ, layer, 0) - b * (sxz - sxz_prior + syz + z_ahead(szz) - szz)
            for f, value in enumerate((rx, rz, syy, raw)[: 4 if step == 0 else 3]):
                to_south[step, pl.ds(4 * f + i, 1), :] = value[0:1]
            k, at = NY // 8 - 1, pl.ds(NY - 8, 8)
            raw = mat_b[i, at, :]
            b = COURANT * raw
            sxy, syy, syz = (tile(f, layer, k) for f in (SXY, SYY, SYZ))
            sxy_prior = tile(SXY, layer - 1, k) if i > 0 else nothing
            ry = tile(VY, layer, k) - b * (sxy - sxy_prior - syy + syz - z_behind(syz))
            for f, value in enumerate((ry, sxy, syz, raw)[: 4 if step == 0 else 3]):
                to_north[step, pl.ds(4 * f + i, 1), :] = value[7:8]
        k = NY // 8 - 1
        to_corner[step, 0, 0:1] = tile(SXY, LAST, k)[7:8]
        to_corner[step, 1, 0:1] = tile(SXX, 1, 0)[0:1]
        to_corner[step, 1, 1:2] = tile(SYY, 1, 0)[0:1]
        to_corner[step, 2, 0:1] = tile(SYZ, 1, k)[7:8]
        to_corner[step, 3, 0:1] = tile(SXZ, LAST, 0)[0:1]

    def halo_copies(step):
        full = 4 if step == 0 else 3
        faces = [
            (to_lo.at[step, pl.ds(0, full)], from_hi.at[step, pl.ds(0, full)], (-1, 0)),
            (to_hi.at[step, pl.ds(0, full)], from_lo.at[step, pl.ds(0, full)], (1, 0)),
            (to_south.at[step], from_north.at[step], (0, -1)),
            (to_north.at[step], from_south.at[step], (0, 1)),
        ]
        for slot, (dx, dy) in enumerate(corners):
            faces.append((to_corner.at[step, slot], from_corner.at[step, slot], (-dx, -dy)))
        return [
            (
                pltpu.make_async_remote_copy(
                    src_ref=src, dst_ref=dst, send_sem=halo_send.at[step, n], recv_sem=halo_recv.at[step, n],
                    device_id={"gx": me + dx, "gy": row + dy}, device_id_type=MESH,
                ),
                exists[(dx, dy)], exists[(-dx, -dy)],
            )
            for n, (src, dst, (dx, dy)) in enumerate(faces)
        ]

    def send_halo(step):
        for copy, there, _ in halo_copies(step):

            @pl.when(there)
            def _():
                copy.start()

    def take_halo(step):
        for copy, _, comes in halo_copies(step):

            @pl.when(comes)
            def _():
                copy.wait_recv()

    def finish_halo(step):
        sxy_ll = from_corner[step, 0, 0:1]
        sxx_hh, syy_hh = from_corner[step, 1, 0:1], from_corner[step, 1, 1:2]
        syz_hl, sxz_lh = from_corner[step, 2, 0:1], from_corner[step, 3, 0:1]
        for k in range(NY // 8):
            at, framed = pl.ds(8 * k, 8), pl.ds(TOP + 8 * k, 8)
            b = COURANT * from_lo[0, 3, at, :]
            vx = from_lo[step, 0, at, :] - b * tile(SXX, 1, k)
            if k == 0:
                vx = jnp.where(rows_of(vx.shape) == 0, vx + b * sxy_ll, vx)
            field[VX, 0, framed, :] = vx
            field[SXY, 0, framed, :] = from_lo[step, 1, at, :]
            field[SXZ, 0, framed, :] = from_lo[step, 2, at, :]
            b = COURANT * from_hi[0, 3, at, :]
            vy = from_hi[step, 0, at, :] + b * tile(SXY, LAST, k)
            vz = from_hi[step, 1, at, :] + b * tile(SXZ, LAST, k)
            if k == NY // 8 - 1:
                vy = jnp.where(rows_of(vy.shape) == 7, vy - b * syy_hh, vy)
            if k == 0:
                vz = jnp.where(rows_of(vz.shape) == 0, vz + b * syz_hl, vz)
            field[VY, LAST + 1, framed, :] = vy
            field[VZ, LAST + 1, framed, :] = vz
            field[SXX, LAST + 1, framed, :] = from_hi[step, 2, at, :]
        for i in range(NX):
            layer = i + 1
            part, sxy, syz = (from_south[step, pl.ds(4 * f + i, 1), :] for f in range(3))
            b = COURANT * from_south[0, pl.ds(12 + i, 1), :]
            vy = part - b * tile(SYY, layer, 0)[0:1]
            if i == 0:
                vy = vy + b * sxy_ll
            field[VY, layer, pl.ds(TOP - 1, 1), :] = vy
            field[SXY, layer, pl.ds(TOP - 1, 1), :] = sxy
            field[SYZ, layer, pl.ds(TOP - 1, 1), :] = syz
            part_x, part_z, syy = (from_north[step, pl.ds(4 * f + i, 1), :] for f in range(3))
            b = COURANT * from_north[0, pl.ds(12 + i, 1), :]
            vx = part_x + b * tile(SXY, layer, NY // 8 - 1)[7:8]
            vz = part_z + b * tile(SYZ, layer, NY // 8 - 1)[7:8]
            if i == NX - 1:
                vx = vx - b * sxx_hh
            if i == 0:
                vz = vz + b * sxz_lh
            field[VX, layer, pl.ds(END, 1), :] = vx
            field[VZ, layer, pl.ds(END, 1), :] = vz
            field[SYY, layer, pl.ds(END, 1), :] = syy

    def dyn(f, layer, start):
        return field[f, layer, pl.ds(start, 8), :]

    def move_velocity(n, _):
        i, k = n // (NY // 8), n % (NY // 8)
        layer, at = i + 1, pl.multiple_of(TOP + 8 * k, 8)
        before, after = pl.multiple_of(8 * k, 8), pl.multiple_of(TOP + 8 + 8 * k, 8)
        b = COURANT * mat_b[i, pl.ds(pl.multiple_of(8 * k, 8), 8), :]
        sxx, syy, szz, sxy, sxz, syz = (dyn(f, layer, at) for f in (SXX, SYY, SZZ, SXY, SXZ, SYZ))
        dx = dyn(SXX, layer + 1, at) - sxx + sxy - y_behind(sxy, dyn(SXY, layer, before)) + sxz - z_behind(sxz)
        field[VX, layer, pl.ds(at, 8), :] = dyn(VX, layer, at) - b * dx
        dy = sxy - dyn(SXY, layer - 1, at) + y_ahead(syy, dyn(SYY, layer, after)) - syy + syz - z_behind(syz)
        field[VY, layer, pl.ds(at, 8), :] = dyn(VY, layer, at) - b * dy
        dz = sxz - dyn(SXZ, layer - 1, at) + syz - y_behind(syz, dyn(SYZ, layer, before)) + z_ahead(szz) - szz
        field[VZ, layer, pl.ds(at, 8), :] = dyn(VZ, layer, at) - b * dz
        return 0

    def move_stress(step, n, _):
        i, k = n // (NY // 8), n % (NY // 8)
        layer, at = i + 1, pl.multiple_of(TOP + 8 * k, 8)
        before, after = pl.multiple_of(8 * k, 8), pl.multiple_of(TOP + 8 + 8 * k, 8)
        flat = pl.ds(pl.multiple_of(8 * k, 8), 8)
        vx, vy, vz = (dyn(f, layer, at) for f in (VX, VY, VZ))
        exx = vx - dyn(VX, layer - 1, at)
        eyy = vy - y_behind(vy, dyn(VY, layer, before))
        ezz = vz - z_behind(vz)
        exy = y_ahead(vx, dyn(VX, layer, after)) - vx + dyn(VY, layer + 1, at) - vy
        exz = z_ahead(vx) - vx + dyn(VZ, layer + 1, at) - vz
        eyz = z_ahead(vy) - vy + y_ahead(vz, dyn(VZ, layer, after)) - vz
        mu = COURANT * mat_m[i, flat, :]
        both = (COURANT * mat_l[i, flat, :]) * (exx + eyy + ezz)
        for f, e in ((SXX, exx), (SYY, eyy), (SZZ, ezz)):
            field[f, layer, pl.ds(at, 8), :] = dyn(f, layer, at) - (both + 2.0 * mu * e)
        for f, e in ((SXY, exy), (SXZ, exz), (SYZ, eyz)):
            field[f, layer, pl.ds(at, 8), :] = dyn(f, layer, at) - mu * e
        for c, e in enumerate((exx, eyy, ezz, exy, exz, eyz)):
            strain[6 * step + c, i, flat, :] = e
        return 0

    loads[0].wait()
    loads[1].wait()
    stage(0)
    loads[2].wait()
    loads[3].wait()
    pl.semaphore_wait(barrier, expected)
    send_halo(0)

    def exchange(peer):
        return pltpu.make_async_remote_copy(
            src_ref=held.at[peer, pl.ds(0, 25)], dst_ref=landed.at[me, pl.ds(0, 25)],
            send_sem=send_sem.at[peer], recv_sem=recv_sem.at[me],
            device_id={"gx": peer}, device_id_type=MESH,
        )

    def launch(t, _):
        exchange(exchange_peer(t)).start()
        return 0

    lax.fori_loop(0, count - 1, launch, 0)
    landed[me] = held[me]
    loads[4].wait()
    loads[5].wait()

    for step in range(2):
        take_halo(step)
        finish_halo(step)
        lax.fori_loop(0, NX * NY // 8, move_velocity, 0)
        lax.fori_loop(0, NX * NY // 8, functools.partial(move_stress, step), 0)
        if step == 0:
            stage(1)
            send_halo(1)

    store = pltpu.make_async_copy(field.at[:, own_x, own_y, :], out, out_sem.at[0])
    store.start()

    def arrive(t, _):
        other = lax.rem(me + t, count)
        pltpu.make_async_remote_copy(
            src_ref=held.at[other, pl.ds(0, 25)], dst_ref=landed.at[other, pl.ds(0, 25)],
            send_sem=send_sem.at[other], recv_sem=recv_sem.at[other],
            device_id={"gx": other}, device_id_type=MESH,
        ).wait()
        return 0

    lax.fori_loop(1, count, arrive, 0)

    def correlate(n, _):
        i, k = n // (NY // 8), n % (NY // 8)
        flat = pl.ds(pl.multiple_of(8 * k, 8), 8)
        holders = [inverse[i * (NY // 2) + 4 * k + r] for r in range(4)]
        pair = rows_of((8, 128)) // 2
        shift = (rows_of((8, 128)) % 2) * 16

        def gathered(line):
            parts = [jnp.broadcast_to(landed[h, pl.ds(line, 1), :], (8, 128)) for h in holders]
            low = jnp.where(pair == 0, parts[0], parts[1])
            high = jnp.where(pair == 2, parts[2], parts[3])
            return jnp.where(pair < 2, low, high)

        scale_rows = gathered(24).astype(jnp.float32) * (1.0 / SCALE_UNIT)

        def stored(c):
            scale = jnp.broadcast_to(scale_rows[:, c : c + 1], (8, 128))
            halves = [gathered(2 * c + half) ^ jnp.int32(-2147483648) for half in range(2)]
            quarters = []
            for extra in (0, 8):
                for word in halves:
                    byte = jnp.right_shift(word, shift + extra) & 255
                    quarters.append((byte.astype(jnp.float32) - 128.0) * scale)
            return jnp.concatenate(quarters, axis=1)

        for_lambda, for_mu = None, None
        for step in range(2):
            e = [strain[6 * step + c, i, flat, :] for c in range(3)]
            trace = e[0] + e[1] + e[2]
            total, twice = None, None
            for c in range(3):
                f = stored(6 * step + c)
                total = f if total is None else total + f
                twice = e[c] * f if twice is None else twice + e[c] * f
            mu = 2.0 * twice
            for c in range(3, 6):
                mu = mu + strain[6 * step + c, i, flat, :] * stored(6 * step + c)
            for_lambda = trace * total if for_lambda is None else for_lambda + trace * total
            for_mu = mu if for_mu is None else for_mu + mu
        grad[0, i, flat, :] = for_lambda
        grad[1, i, flat, :] = for_mu
        return 0

    lax.fori_loop(0, NX * NY // 8, correlate, 0)
    last = pltpu.make_async_copy(grad, gradients, out_sem.at[1])
    last.start()
    for step in range(2):
        for copy, there, _ in halo_copies(step):

            @pl.when(there)
            def _():
                copy.wait_send()

    store.wait()
    last.wait()


def on_device(adjoint, buoyancy, lame_lambda, shear_mu, packed, scales, perm):
    count, rows_gy = lax.axis_size("gx"), lax.axis_size("gy")
    inverse = inverse_order(perm[0])
    words = packed.reshape(count, 24, 128)
    factors = jnp.round(scales[0, :, 0] * SCALE_UNIT).astype(jnp.int32)
    factors = jnp.pad(factors, ((0, 0), (0, 128 - factors.shape[1])))[:, None, :]
    any_space, smem = pl.BlockSpec(memory_space=pl.ANY), pl.BlockSpec(memory_space=pltpu.SMEM)
    f32, i32 = jnp.float32, jnp.int32
    return pl.pallas_call(
        functools.partial(kernel, count, rows_gy),
        out_shape=(
            jax.ShapeDtypeStruct((9, NX, NY, NZ), f32),
            jax.ShapeDtypeStruct((2, NX, NY, NZ), f32),
        ),
        in_specs=[any_space] * 6 + [smem],
        out_specs=(any_space, any_space),
        scratch_shapes=[
            pltpu.VMEM((9, NX + 2, NY + 16, NZ), f32),
            pltpu.VMEM((NX, NY, NZ), f32),
            pltpu.VMEM((NX, NY, NZ), f32),
            pltpu.VMEM((NX, NY, NZ), f32),
            pltpu.VMEM((12, NX, NY, NZ), f32),
            pltpu.VMEM((2, NX, NY, NZ), f32),
            pltpu.VMEM((64, 32, 128), i32),
            pltpu.VMEM((64, 32, 128), i32),
            pltpu.VMEM((2, 4, NY, NZ), f32),
            pltpu.VMEM((2, 4, NY, NZ), f32),
            pltpu.VMEM((2, 16, NZ), f32),
            pltpu.VMEM((2, 16, NZ), f32),
            pltpu.VMEM((2, 4, 2, NZ), f32),
            pltpu.VMEM((2, 4, NY, NZ), f32),
            pltpu.VMEM((2, 4, NY, NZ), f32),
            pltpu.VMEM((2, 16, NZ), f32),
            pltpu.VMEM((2, 16, NZ), f32),
            pltpu.VMEM((2, 4, 2, NZ), f32),
            pltpu.SemaphoreType.DMA((6,)),
            pltpu.SemaphoreType.DMA((64,)),
            pltpu.SemaphoreType.DMA((64,)),
            pltpu.SemaphoreType.DMA((2, 8)),
            pltpu.SemaphoreType.DMA((2, 8)),
            pltpu.SemaphoreType.DMA((2,)),
        ],
        compiler_params=pltpu.CompilerParams(
            collective_id=0, has_side_effects=True, vmem_limit_bytes=40 * 2**20
        ),
    )(adjoint, buoyancy, lame_lambda, shear_mu, words, factors, inverse)


def solution(mesh):
    return jax.shard_map(
        on_device,
        mesh=mesh,
        in_specs=(
            P(None, "gx", "gy", None),
            P("gx", "gy", None),
            P("gx", "gy", None),
            P("gx", "gy", None),
            P("gx", None, "gy", None, None),
            P("gx", None, "gy", None),
            P("gx", None),
        ),
        out_specs=(P(None, "gx", "gy", None), P(None, "gx", "gy", None)),
        check_vma=False,
    )
```

time: 203 us -> 69.6 us (0.34)
  the two profiles are of different devices: /device:TPU:34 before, /device:TPU:2 now
where the time goes in v1:
time: 69.6 us; the launch traced here: 69.3 us
  Pallas kernels  59.2 us (85%)
  local copies, waits for them, and re-layouts  8.64 us (12%)
  other arithmetic  0.77 us (1%)
    pallas_call x1, Pallas kernels, on_device(): pl.pallas_call(functools.partial(kernel, count, rows_gy), out_shape=(jax....  59.2 us
    unnamed x13, local copies, waits for them, and re-layouts  8.63 us

profile of v1, /device:TPU:2, one launch (start us, length us, event | category | flops | bytes accessed | tf_op | source)
XLA Modules:
  0.0 69.3 jit_solution(10523382459336237367)
XLA Ops:
  0.6 0.8 %select_reduce_fusion.inverse = s32[64]{0:T(128)S(1)} fusion(s32[64]{0:T(128)} %bitcast.7), kind=kLoop, calls=%fused_computation | loop fusion | flops 12224 | bytes 512 | tf_op jit(solution)/shard_map/reduce_sum | solution.py:23
  1.4 0.8 %copy.10 = f32[1,64,1,12]{3,1,2,0:T(8,128)S(1)} copy(f32[1,64,1,12]{1,2,3,0:T(1,128)} %param.12) | data formatting | bytes 6144 | tf_op args[5]
  2.2 0.0 copy-start
  2.2 1.7 %copy-done = f32[9,4,32,512]{3,2,1,0:T(8,128)S(1)} copy-done((f32[9,4,32,512]{3,2,1,0:T(8,128)S(1)}, f32[9,4,32,512]{3,2,1,0:T(8,128)}, u32[]{:S(2)}) %copy-start) | copy-done | bytes 2359320
  3.9 0.0 copy-start.1
  3.9 1.1 %copy-done.1 = s32[1,64,1,12,256]{4,2,3,1,0:T(1,128)S(1)} copy-done((s32[1,64,1,12,256]{4,2,3,1,0:T(1,128)S(1)}, s32[1,64,1,12,256]{4,2,3,1,0:T(1,128)}, u32[]{:S(2)}) %copy-start.1) | copy-done | bytes 786456
  5.0 0.0 copy-start.2
  5.0 0.9 %copy-done.2 = f32[4,32,512]{2,1,0:T(8,128)S(1)} copy-done((f32[4,32,512]{2,1,0:T(8,128)S(1)}, f32[4,32,512]{2,1,0:T(8,128)}, u32[]{:S(2)}) %copy-start.2) | copy-done | bytes 262168
  6.0 0.0 copy-start.3
  6.0 0.9 %copy-done.3 = f32[4,32,512]{2,1,0:T(8,128)S(1)} copy-done((f32[4,32,512]{2,1,0:T(8,128)S(1)}, f32[4,32,512]{2,1,0:T(8,128)}, u32[]{:S(2)}) %copy-start.3) | copy-done | bytes 262168
  6.9 0.0 copy-start.4
  6.9 0.9 %copy-done.4 = f32[4,32,512]{2,1,0:T(8,128)S(1)} copy-done((f32[4,32,512]{2,1,0:T(8,128)S(1)}, f32[4,32,512]{2,1,0:T(8,128)}, u32[]{:S(2)}) %copy-start.4) | copy-done | bytes 262168
  7.9 59.2 %shard_map.86 = (f32[9,4,32,512]{3,2,1,0:T(8,128)S(1)}, f32[2,4,32,512]{3,2,1,0:T(8,128)S(1)}) custom-call(f32[9,4,32,512]{3,2,1,0:T(8,128)S(1)} %copy-done, f32[4,32,512]{2,1,0:T(8,128)S(1)} %copy-done.2, f32[4,32,512]{2,1,0:T(8,128)S(1)} %copy-done.3, f32[4,32,512]{2,1,0:T(8,128)S(1)} %copy-done.4, s32[64,24,128]{2,1,0:T(8,128)S(1)} %bitcast.5, ...), custom_call_target="tpu_custom_call" | custom-call | tf_op jit(solution)/shard_map/pallas_call | solution.py:406
  67.1 1.4 %copy.13 = f32[9,4,32,512]{3,2,1,0:T(8,128)} copy(f32[9,4,32,512]{3,2,1,0:T(8,128)S(1)} %get-tuple-element.4) | data formatting | bytes 4718592
  68.5 0.8 %copy.14 = f32[2,4,32,512]{3,2,1,0:T(8,128)} copy(f32[2,4,32,512]{3,2,1,0:T(8,128)S(1)} %get-tuple-element.5) | data formatting | bytes 1048576
  (2 shorter events, 0.0 us)
Async XLA Ops:
  2.2 1.7 %copy-start = (f32[9,4,32,512]{3,2,1,0:T(8,128)S(1)}, f32[9,4,32,512]{3,2,1,0:T(8,128)}, u32[]{:S(2)}) copy-start(f32[9,4,32,512]{3,2,1,0:T(8,128)} %adjoint.1) | copy-start | bytes 7077892
  3.9 1.1 %copy-start.1 = (s32[1,64,1,12,256]{4,2,3,1,0:T(1,128)S(1)}, s32[1,64,1,12,256]{4,2,3,1,0:T(1,128)}, u32[]{:S(2)}) copy-start(s32[1,64,1,12,256]{4,2,3,1,0:T(1,128)} %param.11) | copy-start | bytes 2359300
  5.0 0.9 %copy-start.2 = (f32[4,32,512]{2,1,0:T(8,128)S(1)}, f32[4,32,512]{2,1,0:T(8,128)}, u32[]{:S(2)}) copy-start(f32[4,32,512]{2,1,0:T(8,128)} %buoyancy.1) | copy-start | bytes 786436
  6.0 0.9 %copy-start.3 = (f32[4,32,512]{2,1,0:T(8,128)S(1)}, f32[4,32,512]{2,1,0:T(8,128)}, u32[]{:S(2)}) copy-start(f32[4,32,512]{2,1,0:T(8,128)} %lame.1) | copy-start | bytes 786436
  6.9 0.9 %copy-start.4 = (f32[4,32,512]{2,1,0:T(8,128)S(1)}, f32[4,32,512]{2,1,0:T(8,128)}, u32[]{:S(2)}) copy-start(f32[4,32,512]{2,1,0:T(8,128)} %shear.1) | copy-start | bytes 786436

commit v2 on v1

--- a/solution.py
+++ b/solution.py
@@ -16,13 +16,6 @@
 SCALE_UNIT = 2.0**31
 
 
-def inverse_order(row):
-    count = row.shape[0]
-    slots = jnp.arange(count, dtype=jnp.int32)
-    hits = (row[None, :] == slots[:, None]).astype(jnp.int32)
-    return jnp.sum(hits * slots[None, :], axis=1)
-
-
 def rows_of(shape):
     return lax.broadcasted_iota(jnp.int32, shape, 0)
 
@@ -49,12 +42,13 @@
 
 def kernel(
     count, rows_gy,
-    adjoint, buoyancy, lame, shear, words, factors, inverse,
+    adjoint, buoyancy, lame, shear, words, factors, order,
     out, gradients,
-    field, mat_b, mat_l, mat_m, strain, grad, held, landed,
+    field, mat_b, mat_l, mat_m, strain, held, landed,
     to_lo, to_hi, to_south, to_north, to_corner,
     from_lo, from_hi, from_south, from_north, from_corner,
-    load_sem, send_sem, recv_sem, halo_send, halo_recv, out_sem,
+    square, factor_rows, order_row, inverse_row, inverse,
+    load_sem, send_sem, recv_sem, halo_send, halo_recv, out_sem, ready,
 ):
     me, row = lax.axis_index("gx"), lax.axis_index("gy")
     own_x, own_y = pl.ds(1, NX), pl.ds(TOP, NY)
@@ -65,20 +59,25 @@
         pltpu.make_async_copy(adjoint, field.at[:, own_x, own_y, :], load_sem.at[0]),
         pltpu.make_async_copy(buoyancy, mat_b, load_sem.at[1]),
         pltpu.make_async_copy(words, held.at[:, pl.ds(0, 24), :], load_sem.at[2]),
-        pltpu.make_async_copy(factors, held.at[:, pl.ds(24, 1), :], load_sem.at[3]),
+        pltpu.make_async_copy(factors, factor_rows, load_sem.at[3]),
         pltpu.make_async_copy(lame, mat_l, load_sem.at[4]),
         pltpu.make_async_copy(shear, mat_m, load_sem.at[5]),
+        pltpu.make_async_copy(order, order_row, load_sem.at[6]),
     ]
     for load in loads:
         load.start()
 
-    def exchange_peer(t):
-        far = 1 - t % 2
-        u = t // 2 + (1 - far)
-        x, z, y, core = me // 16, (me // 8) % 2, (me // 2) % 4, me % 2
-        return (
-            ((x + u // 8) % 4) * 16 + ((z + far) % 2) * 8 + ((y + (u // 2) % 4) % 4) * 2 + (core + u % 2) % 2
-        )
+    x, z, y, core = me // 16, (me // 8) % 2, (me // 2) % 4, me % 2
+    at_x = [((x + d) % 4) * 16 for d in range(4)]
+    at_z = [((z + d) % 2) * 8 for d in range(2)]
+    at_y = [((y + d) % 4) * 2 for d in range(4)]
+    at_core = [(core + d) % 2 for d in range(2)]
+
+    def peer(dx, dz, dy, dcore):
+        return at_x[dx] + at_z[dz] + at_y[dy] + at_core[dcore]
+
+    def signal(sem, device):
+        pl.semaphore_signal(sem, inc=1, device_id=device, device_id_type=MESH)
 
     exists = {
         (-1, 0): has_lo, (1, 0): has_hi, (0, -1): has_south, (0, 1): has_north,
@@ -88,21 +87,19 @@
 
     barrier = pltpu.get_barrier_semaphore()
 
-    def greet(t, _):
-        pl.semaphore_signal(barrier, inc=1, device_id={"gx": exchange_peer(t)}, device_id_type=MESH)
-        return 0
-
-    lax.fori_loop(0, count - 1, greet, 0)
-    expected = jnp.int32(count - 1)
+    along_x = [peer(d, 0, 0, 0) for d in (1, 2, 3)]
+    along_y = [peer(0, 0, d, 0) for d in (1, 2, 3)]
+    across_z, across_core = peer(0, 1, 0, 0), peer(0, 0, 0, 1)
+    lines = [across_z] + along_x + along_y + [across_core]
+    for other in lines:
+        signal(barrier, {"gx": other})
+    expected = jnp.int32(len(lines))
     for (dx, dy), there in exists.items():
-        if dy != 0:
-            expected = expected + there.astype(jnp.int32)
-
-            @pl.when(there)
-            def _():
-                pl.semaphore_signal(
-                    barrier, inc=1, device_id={"gx": me + dx, "gy": row + dy}, device_id_type=MESH
-                )
+        expected = expected + there.astype(jnp.int32)
+
+        @pl.when(there)
+        def _():
+            signal(barrier, {"gx": me + dx, "gy": row + dy})
 
     for there, ref in ((has_lo, from_lo), (has_hi, from_hi), (has_south, from_south), (has_north, from_north)):
 
@@ -291,27 +288,57 @@
             strain[6 * step + c, i, flat, :] = e
         return 0
 
+    def prepare_blocks():
+        loads[3].wait()
+        loads[2].wait()
+        for c in range(12):
+            square[pl.ds(c, 1), 0:64] = factor_rows[c]
+        turned = jnp.round(square[...].T * SCALE_UNIT).astype(jnp.int32)
+        for owner in range(64):
+            held[owner, 24:25, :] = turned[owner : owner + 1]
+        places = jnp.broadcast_to(square[16:17, :], (128, 128)).T
+        hits = places == lanes_of((128, 128)).astype(jnp.float32)
+        found = jnp.sum(jnp.where(hits, rows_of((128, 128)), 0), axis=0, keepdims=True)
+        inverse_row[...] = found
+
     loads[0].wait()
     loads[1].wait()
     stage(0)
-    loads[2].wait()
-    loads[3].wait()
+
+    def exchange(other):
+        return pltpu.make_async_remote_copy(
+            src_ref=held.at[other, pl.ds(0, 25)], dst_ref=landed.at[me, pl.ds(0, 25)],
+            send_sem=send_sem.at[other], recv_sem=recv_sem.at[me],
+            device_id={"gx": other}, device_id_type=MESH,
+        )
+
+    def send_plane(dz, dcore):
+        for dx in range(4):
+            for dy in range(4):
+                if (dx, dz, dy, dcore) != (0, 0, 0, 0):
+                    exchange(peer(dx, dz, dy, dcore)).start()
+
     pl.semaphore_wait(barrier, expected)
     send_halo(0)
-
-    def exchange(peer):
-        return pltpu.make_async_remote_copy(
-            src_ref=held.at[peer, pl.ds(0, 25)], dst_ref=landed.at[me, pl.ds(0, 25)],
-            send_sem=send_sem.at[peer], recv_sem=recv_sem.at[me],
-            device_id={"gx": peer}, device_id_type=MESH,
-        )
-
-    def launch(t, _):
-        exchange(exchange_peer(t)).start()
-        return 0
-
-    lax.fori_loop(0, count - 1, launch, 0)
+    for other in along_x:
+        signal(ready.at[0], {"gx": other})
+    square[...] = jnp.full((128, 128), 999.0, jnp.float32)
+    loads[6].wait()
+    square[16:17, 0:64] = order_row[...].astype(jnp.float32)
+    prepare_blocks()
     landed[me] = held[me]
+    to_smem = pltpu.make_async_copy(inverse_row, inverse, load_sem.at[7])
+    to_smem.start()
+    pl.semaphore_wait(ready.at[0], 3)
+    signal(ready.at[1], {"gx": across_z})
+    signal(ready.at[1], {"gx": across_core})
+    send_plane(0, 0)
+    pl.semaphore_wait(ready.at[1], 2)
+    signal(ready.at[2], {"gx": across_core})
+    send_plane(1, 0)
+    send_plane(0, 1)
+    pl.semaphore_wait(ready.at[2], 1)
+    send_plane(1, 1)
     loads[4].wait()
     loads[5].wait()
 
@@ -337,11 +364,12 @@
         return 0
 
     lax.fori_loop(1, count, arrive, 0)
+    to_smem.wait()
 
     def correlate(n, _):
         i, k = n // (NY // 8), n % (NY // 8)
         flat = pl.ds(pl.multiple_of(8 * k, 8), 8)
-        holders = [inverse[i * (NY // 2) + 4 * k + r] for r in range(4)]
+        holders = [jnp.clip(inverse[0, i * (NY // 2) + 4 * k + r], 0, count - 1) for r in range(4)]
         pair = rows_of((8, 128)) // 2
         shift = (rows_of((8, 128)) % 2) * 16
 
@@ -377,13 +405,11 @@
                 mu = mu + strain[6 * step + c, i, flat, :] * stored(6 * step + c)
             for_lambda = trace * total if for_lambda is None else for_lambda + trace * total
             for_mu = mu if for_mu is None else for_mu + mu
-        grad[0, i, flat, :] = for_lambda
-        grad[1, i, flat, :] = for_mu
+        gradients[0, i, flat, :] = for_lambda
+        gradients[1, i, flat, :] = for_mu
         return 0
 
     lax.fori_loop(0, NX * NY // 8, correlate, 0)
-    last = pltpu.make_async_copy(grad, gradients, out_sem.at[1])
-    last.start()
     for step in range(2):
         for copy, there, _ in halo_copies(step):
 
@@ -392,32 +418,41 @@
                 copy.wait_send()
 
     store.wait()
-    last.wait()
+
+
+def hand_over(state, grad, out, gradients, sem):
+    copies = [
+        pltpu.make_async_copy(state, out, sem.at[0]),
+        pltpu.make_async_copy(grad, gradients, sem.at[1]),
+    ]
+    for copy in copies:
+        copy.start()
+    for copy in copies:
+        copy.wait()
 
 
 def on_device(adjoint, buoyancy, lame_lambda, shear_mu, packed, scales, perm):
     count, rows_gy = lax.axis_size("gx"), lax.axis_size("gy")
-    inverse = inverse_order(perm[0])
     words = packed.reshape(count, 24, 128)
-    factors = jnp.round(scales[0, :, 0] * SCALE_UNIT).astype(jnp.int32)
-    factors = jnp.pad(factors, ((0, 0), (0, 128 - factors.shape[1])))[:, None, :]
-    any_space, smem = pl.BlockSpec(memory_space=pl.ANY), pl.BlockSpec(memory_space=pltpu.SMEM)
+    factors = jnp.transpose(scales[0], (2, 1, 0))
+    any_space, in_vmem = pl.BlockSpec(memory_space=pl.ANY), pl.BlockSpec(memory_space=pltpu.VMEM)
     f32, i32 = jnp.float32, jnp.int32
-    return pl.pallas_call(
+    inputs = (adjoint, buoyancy, lame_lambda, shear_mu, words, factors, perm)
+    inputs = [pltpu.with_memory_space_constraint(x, pltpu.HBM) for x in inputs]
+    state, grad = pl.pallas_call(
         functools.partial(kernel, count, rows_gy),
         out_shape=(
-            jax.ShapeDtypeStruct((9, NX, NY, NZ), f32),
-            jax.ShapeDtypeStruct((2, NX, NY, NZ), f32),
+            pltpu.VMEM((9, NX, NY, NZ), f32),
+            pltpu.VMEM((2, NX, NY, NZ), f32),
         ),
-        in_specs=[any_space] * 6 + [smem],
-        out_specs=(any_space, any_space),
+        in_specs=[any_space] * 7,
+        out_specs=(any_space, in_vmem),
         scratch_shapes=[
             pltpu.VMEM((9, NX + 2, NY + 16, NZ), f32),
             pltpu.VMEM((NX, NY, NZ), f32),
             pltpu.VMEM((NX, NY, NZ), f32),
             pltpu.VMEM((NX, NY, NZ), f32),
             pltpu.VMEM((12, NX, NY, NZ), f32),
-            pltpu.VMEM((2, NX, NY, NZ), f32),
             pltpu.VMEM((64, 32, 128), i32),
             pltpu.VMEM((64, 32, 128), i32),
             pltpu.VMEM((2, 4, NY, NZ), f32),
@@ -430,17 +465,33 @@
             pltpu.VMEM((2, 16, NZ), f32),
             pltpu.VMEM((2, 16, NZ), f32),
             pltpu.VMEM((2, 4, 2, NZ), f32),
-            pltpu.SemaphoreType.DMA((6,)),
+            pltpu.VMEM((128, 128), f32),
+            pltpu.VMEM((12, 1, 64), f32),
+            pltpu.VMEM((1, 64), i32),
+            pltpu.VMEM((1, 128), i32),
+            pltpu.SMEM((1, 128), i32),
+            pltpu.SemaphoreType.DMA((8,)),
             pltpu.SemaphoreType.DMA((64,)),
             pltpu.SemaphoreType.DMA((64,)),
             pltpu.SemaphoreType.DMA((2, 8)),
             pltpu.SemaphoreType.DMA((2, 8)),
             pltpu.SemaphoreType.DMA((2,)),
+            pltpu.SemaphoreType.REGULAR((3,)),
         ],
         compiler_params=pltpu.CompilerParams(
-            collective_id=0, has_side_effects=True, vmem_limit_bytes=40 * 2**20
+            collective_id=0, has_side_effects=True, vmem_limit_bytes=32 * 2**20
         ),
-    )(adjoint, buoyancy, lame_lambda, shear_mu, words, factors, inverse)
+    )(*inputs)
+    return pl.pallas_call(
+        hand_over,
+        out_shape=(
+            jax.ShapeDtypeStruct((9, NX, NY, NZ), f32),
+            jax.ShapeDtypeStruct((2, NX, NY, NZ), f32),
+        ),
+        in_specs=[any_space] * 2,
+        out_specs=(any_space, any_space),
+        scratch_shapes=[pltpu.SemaphoreType.DMA((2,))],
+    )(*(pltpu.with_memory_space_constraint(x, pltpu.VMEM) for x in (state, grad)))
 
 
 def solution(mesh):

time: 69.6 us -> 51.3 us (0.74)
  the two profiles are of different devices: /device:TPU:2 before, /device:TPU:34 now
where the time goes in v2:
time: 51.3 us; the launch traced here: 51.2 us
  Pallas kernels  50.5 us (98%)
  between operations  0.64 us (1%)
    pallas_call x1, Pallas kernels, on_device(): pl.pallas_call(functools.partial(kernel, count, rows_gy), out_shape=(pltp...  49 us
    pallas_call x1, Pallas kernels, on_device(): pl.pallas_call(hand_over, out_shape=(jax.ShapeDtypeStruct((9, NX, NY, NZ)...  1.59 us

profile of v2, /device:TPU:34, one launch (start us, length us, event | category | flops | bytes accessed | tf_op | source)
XLA Modules:
  0.0 51.2 jit_solution(5430491402794560782)
XLA Ops:
  0.6 49.0 %shard_map.86 = (f32[9,4,32,512]{3,2,1,0:T(8,128)S(1)}, f32[2,4,32,512]{3,2,1,0:T(8,128)S(1)}) custom-call(f32[9,4,32,512]{3,2,1,0:T(8,128)} %adjoint.1, f32[4,32,512]{2,1,0:T(8,128)} %buoyancy.1, f32[4,32,512]{2,1,0:T(8,128)} %lame.1, f32[4,32,512]{2,1,0:T(8,128)} %shear.1, s32[64,24,128]{2,1,0:T(8,128)} %bitcast.4, f32[12,1,64]{2,1,0:T(1,128)} %bitcast.5, ...), custom_call_target="tpu_custom_call" | custom-call | tf_op jit(solution)/shard_map/pallas_call | solution.py:442
  49.6 1.6 %shard_map.87 = (f32[9,4,32,512]{3,2,1,0:T(8,128)}, f32[2,4,32,512]{3,2,1,0:T(8,128)}) custom-call(f32[9,4,32,512]{3,2,1,0:T(8,128)S(1)} %get-tuple-element.4.state, f32[2,4,32,512]{3,2,1,0:T(8,128)S(1)} %get-tuple-element.5.grad), custom_call_target="tpu_custom_call" | custom-call | tf_op jit(solution)/shard_map/pallas_call | solution.py:485

commit v3 on v2

--- a/solution.py
+++ b/solution.py
@@ -44,11 +44,11 @@
     count, rows_gy,
     adjoint, buoyancy, lame, shear, words, factors, order,
     out, gradients,
-    field, mat_b, mat_l, mat_m, strain, held, landed,
+    field, mat_b, mat_l, mat_m, strain, stored, held, landed,
     to_lo, to_hi, to_south, to_north, to_corner,
     from_lo, from_hi, from_south, from_north, from_corner,
     square, factor_rows, order_row, inverse_row, inverse,
-    load_sem, send_sem, recv_sem, halo_send, halo_recv, out_sem, ready,
+    load_sem, send_sem, recv_sem, halo_send, halo_recv, ready,
 ):
     me, row = lax.axis_index("gx"), lax.axis_index("gy")
     own_x, own_y = pl.ds(1, NX), pl.ds(TOP, NY)
@@ -120,7 +120,7 @@
 
     nothing = jnp.zeros((8, NZ), jnp.float32)
 
-    def stage(step):
+    def stage_layers(step):
         for k in range(NY // 8):
             at = pl.ds(8 * k, 8)
             b = COURANT * mat_b[0, at, :]
@@ -143,6 +143,8 @@
             if step == 0:
                 to_lo[0, 3, at, :] = mat_b[0, at, :]
                 to_hi[0, 3, at, :] = mat_b[NX - 1, at, :]
+
+    def stage_rows(step):
         for i in range(NX):
             layer, at = i + 1, pl.ds(0, 8)
             raw = mat_b[i, at, :]
@@ -169,7 +171,7 @@
         to_corner[step, 2, 0:1] = tile(SYZ, 1, k)[7:8]
         to_corner[step, 3, 0:1] = tile(SXZ, LAST, 0)[0:1]
 
-    def halo_copies(step):
+    def halo_copies(step, which=slice(None)):
         full = 4 if step == 0 else 3
         faces = [
             (to_lo.at[step, pl.ds(0, full)], from_hi.at[step, pl.ds(0, full)], (-1, 0)),
@@ -187,11 +189,11 @@
                 ),
                 exists[(dx, dy)], exists[(-dx, -dy)],
             )
-            for n, (src, dst, (dx, dy)) in enumerate(faces)
+            for n, (src, dst, (dx, dy)) in list(enumerate(faces))[which]
         ]
 
-    def send_halo(step):
-        for copy, there, _ in halo_copies(step):
+    def send_halo(step, which):
+        for copy, there, _ in halo_copies(step, which):
 
             @pl.when(there)
             def _():
@@ -215,8 +217,9 @@
             if k == 0:
                 vx = jnp.where(rows_of(vx.shape) == 0, vx + b * sxy_ll, vx)
             field[VX, 0, framed, :] = vx
-            field[SXY, 0, framed, :] = from_lo[step, 1, at, :]
-            field[SXZ, 0, framed, :] = from_lo[step, 2, at, :]
+            b = COURANT * mat_b[0, at, :]
+            field[VY, 1, framed, :] = tile(VY, 1, k) + b * from_lo[step, 1, at, :]
+            field[VZ, 1, framed, :] = tile(VZ, 1, k) + b * from_lo[step, 2, at, :]
             b = COURANT * from_hi[0, 3, at, :]
             vy = from_hi[step, 0, at, :] + b * tile(SXY, LAST, k)
             vz = from_hi[step, 1, at, :] + b * tile(SXZ, LAST, k)
@@ -226,28 +229,32 @@
                 vz = jnp.where(rows_of(vz.shape) == 0, vz + b * syz_hl, vz)
             field[VY, LAST + 1, framed, :] = vy
             field[VZ, LAST + 1, framed, :] = vz
-            field[SXX, LAST + 1, framed, :] = from_hi[step, 2, at, :]
+            b = COURANT * mat_b[NX - 1, at, :]
+            field[VX, LAST, framed, :] = tile(VX, LAST, k) - b * from_hi[step, 2, at, :]
+        first, final = pl.ds(TOP, 1), pl.ds(END - 1, 1)
         for i in range(NX):
             layer = i + 1
             part, sxy, syz = (from_south[step, pl.ds(4 * f + i, 1), :] for f in range(3))
             b = COURANT * from_south[0, pl.ds(12 + i, 1), :]
-            vy = part - b * tile(SYY, layer, 0)[0:1]
+            vy = part - b * field[SYY, layer, first, :]
             if i == 0:
                 vy = vy + b * sxy_ll
             field[VY, layer, pl.ds(TOP - 1, 1), :] = vy
-            field[SXY, layer, pl.ds(TOP - 1, 1), :] = sxy
-            field[SYZ, layer, pl.ds(TOP - 1, 1), :] = syz
+            b = COURANT * mat_b[i, 0:1, :]
+            field[VX, layer, first, :] = field[VX, layer, first, :] + b * sxy
+            field[VZ, layer, first, :] = field[VZ, layer, first, :] + b * syz
             part_x, part_z, syy = (from_north[step, pl.ds(4 * f + i, 1), :] for f in range(3))
             b = COURANT * from_north[0, pl.ds(12 + i, 1), :]
-            vx = part_x + b * tile(SXY, layer, NY // 8 - 1)[7:8]
-            vz = part_z + b * tile(SYZ, layer, NY // 8 - 1)[7:8]
+            vx = part_x + b * field[SXY, layer, final, :]
+            vz = part_z + b * field[SYZ, layer, final, :]
             if i == NX - 1:
                 vx = vx - b * sxx_hh
             if i == 0:
                 vz = vz + b * sxz_lh
             field[VX, layer, pl.ds(END, 1), :] = vx
             field[VZ, layer, pl.ds(END, 1), :] = vz
-            field[SYY, layer, pl.ds(END, 1), :] = syy
+            b = COURANT * mat_b[i, NY - 1 : NY, :]
+            field[VY, layer, final, :] = field[VY, layer, final, :] - b * syy
 
     def dyn(f, layer, start):
         return field[f, layer, pl.ds(start, 8), :]
@@ -266,8 +273,8 @@
         field[VZ, layer, pl.ds(at, 8), :] = dyn(VZ, layer, at) - b * dz
         return 0
 
-    def move_stress(step, n, _):
-        i, k = n // (NY // 8), n % (NY // 8)
+    def move_stress(step, first_layer, stride, n, _):
+        i, k = first_layer + stride * (n // (NY // 8)), n % (NY // 8)
         layer, at = i + 1, pl.multiple_of(TOP + 8 * k, 8)
         before, after = pl.multiple_of(8 * k, 8), pl.multiple_of(TOP + 8 + 8 * k, 8)
         flat = pl.ds(pl.multiple_of(8 * k, 8), 8)
@@ -280,13 +287,29 @@
         eyz = z_ahead(vy) - vy + y_ahead(vz, dyn(VZ, layer, after)) - vz
         mu = COURANT * mat_m[i, flat, :]
         both = (COURANT * mat_l[i, flat, :]) * (exx + eyy + ezz)
-        for f, e in ((SXX, exx), (SYY, eyy), (SZZ, ezz)):
-            field[f, layer, pl.ds(at, 8), :] = dyn(f, layer, at) - (both + 2.0 * mu * e)
-        for f, e in ((SXY, exy), (SXZ, exz), (SYZ, eyz)):
-            field[f, layer, pl.ds(at, 8), :] = dyn(f, layer, at) - mu * e
-        for c, e in enumerate((exx, eyy, ezz, exy, exz, eyz)):
-            strain[6 * step + c, i, flat, :] = e
+        moved = [dyn(f, layer, at) - (both + 2.0 * mu * e) for f, e in ((SXX, exx), (SYY, eyy), (SZZ, ezz))]
+        moved += [dyn(f, layer, at) - mu * e for f, e in ((SXY, exy), (SXZ, exz), (SYZ, eyz))]
+        e = (exx, eyy, ezz, exy, exz, eyz)
+        if step == 0:
+            for f in range(6):
+                field[SXX + f, layer, pl.ds(at, 8), :] = moved[f]
+                strain[f, i, flat, :] = e[f]
+            return 0
+        for f, value in enumerate([vx, vy, vz] + moved):
+            out[f, i, flat, :] = value
+        f = [stored[c, i, flat, :] for c in range(6)]
+        gradients[0, i, flat, :] += (exx + eyy + ezz) * (f[0] + f[1] + f[2])
+        gradients[1, i, flat, :] += 2.0 * (exx * f[0] + eyy * f[1] + ezz * f[2]) + exy * f[3] + exz * f[4] + eyz * f[5]
         return 0
+
+    blank = jnp.zeros((NY, NZ), jnp.float32)
+    field[SXX, LAST + 1, pl.ds(TOP, NY), :] = blank
+    field[SXY, 0, pl.ds(TOP, NY), :] = blank
+    field[SXZ, 0, pl.ds(TOP, NY), :] = blank
+    for layer in range(1, NX + 1):
+        field[SYY, layer, pl.ds(END, 8), :] = nothing
+        field[SXY, layer, 0:TOP, :] = nothing
+        field[SYZ, layer, 0:TOP, :] = nothing
 
     def prepare_blocks():
         loads[3].wait()
@@ -303,7 +326,8 @@
 
     loads[0].wait()
     loads[1].wait()
-    stage(0)
+    stage_layers(0)
+    stage_rows(0)
 
     def exchange(other):
         return pltpu.make_async_remote_copy(
@@ -319,7 +343,7 @@
                     exchange(peer(dx, dz, dy, dcore)).start()
 
     pl.semaphore_wait(barrier, expected)
-    send_halo(0)
+    send_halo(0, slice(None))
     for other in along_x:
         signal(ready.at[0], {"gx": other})
     square[...] = jnp.full((128, 128), 999.0, jnp.float32)
@@ -342,18 +366,6 @@
     loads[4].wait()
     loads[5].wait()
 
-    for step in range(2):
-        take_halo(step)
-        finish_halo(step)
-        lax.fori_loop(0, NX * NY // 8, move_velocity, 0)
-        lax.fori_loop(0, NX * NY // 8, functools.partial(move_stress, step), 0)
-        if step == 0:
-            stage(1)
-            send_halo(1)
-
-    store = pltpu.make_async_copy(field.at[:, own_x, own_y, :], out, out_sem.at[0])
-    store.start()
-
     def arrive(t, _):
         other = lax.rem(me + t, count)
         pltpu.make_async_remote_copy(
@@ -363,9 +375,6 @@
         ).wait()
         return 0
 
-    lax.fori_loop(1, count, arrive, 0)
-    to_smem.wait()
-
     def correlate(n, _):
         i, k = n // (NY // 8), n % (NY // 8)
         flat = pl.ds(pl.multiple_of(8 * k, 8), 8)
@@ -381,7 +390,7 @@
 
         scale_rows = gathered(24).astype(jnp.float32) * (1.0 / SCALE_UNIT)
 
-        def stored(c):
+        def block_values(c):
             scale = jnp.broadcast_to(scale_rows[:, c : c + 1], (8, 128))
             halves = [gathered(2 * c + half) ^ jnp.int32(-2147483648) for half in range(2)]
             quarters = []
@@ -391,33 +400,39 @@
                     quarters.append((byte.astype(jnp.float32) - 128.0) * scale)
             return jnp.concatenate(quarters, axis=1)
 
-        for_lambda, for_mu = None, None
-        for step in range(2):
-            e = [strain[6 * step + c, i, flat, :] for c in range(3)]
-            trace = e[0] + e[1] + e[2]
-            total, twice = None, None
-            for c in range(3):
-                f = stored(6 * step + c)
-                total = f if total is None else total + f
-                twice = e[c] * f if twice is None else twice + e[c] * f
-            mu = 2.0 * twice
-            for c in range(3, 6):
-                mu = mu + strain[6 * step + c, i, flat, :] * stored(6 * step + c)
-            for_lambda = trace * total if for_lambda is None else for_lambda + trace * total
-            for_mu = mu if for_mu is None else for_mu + mu
-        gradients[0, i, flat, :] = for_lambda
-        gradients[1, i, flat, :] = for_mu
+        e = [strain[c, i, flat, :] for c in range(6)]
+        f = [block_values(c) for c in range(6)]
+        gradients[0, i, flat, :] = (e[0] + e[1] + e[2]) * (f[0] + f[1] + f[2])
+        gradients[1, i, flat, :] = (
+            2.0 * (e[0] * f[0] + e[1] * f[1] + e[2] * f[2]) + e[3] * f[3] + e[4] * f[4] + e[5] * f[5]
+        )
+        for c in range(6):
+            stored[c, i, flat, :] = block_values(6 + c)
         return 0
 
-    lax.fori_loop(0, NX * NY // 8, correlate, 0)
+    tiles = NX * NY // 8
+    lax.fori_loop(0, tiles, move_velocity, 0)
+    take_halo(0)
+    finish_halo(0)
+    lax.fori_loop(0, tiles // 2, functools.partial(move_stress, 0, 0, NX - 1), 0)
+    stage_layers(1)
+    send_halo(1, slice(0, 2))
+    lax.fori_loop(0, tiles // 2, functools.partial(move_stress, 0, 1, 1), 0)
+    stage_rows(1)
+    send_halo(1, slice(2, None))
+    lax.fori_loop(0, tiles, move_velocity, 0)
+    lax.fori_loop(1, count, arrive, 0)
+    to_smem.wait()
+    lax.fori_loop(0, tiles, correlate, 0)
+    take_halo(1)
+    finish_halo(1)
+    lax.fori_loop(0, tiles, functools.partial(move_stress, 1, 0, 1), 0)
     for step in range(2):
         for copy, there, _ in halo_copies(step):
 
             @pl.when(there)
             def _():
                 copy.wait_send()
-
-    store.wait()
 
 
 def hand_over(state, grad, out, gradients, sem):
@@ -446,13 +461,14 @@
             pltpu.VMEM((2, NX, NY, NZ), f32),
         ),
         in_specs=[any_space] * 7,
-        out_specs=(any_space, in_vmem),
+        out_specs=(in_vmem, in_vmem),
         scratch_shapes=[
             pltpu.VMEM((9, NX + 2, NY + 16, NZ), f32),
             pltpu.VMEM((NX, NY, NZ), f32),
             pltpu.VMEM((NX, NY, NZ), f32),
             pltpu.VMEM((NX, NY, NZ), f32),
-            pltpu.VMEM((12, NX, NY, NZ), f32),
+            pltpu.VMEM((6, NX, NY, NZ), f32),
+            pltpu.VMEM((6, NX, NY, NZ), f32),
             pltpu.VMEM((64, 32, 128), i32),
             pltpu.VMEM((64, 32, 128), i32),
             pltpu.VMEM((2, 4, NY, NZ), f32),
@@ -475,7 +491,6 @@
             pltpu.SemaphoreType.DMA((64,)),
             pltpu.SemaphoreType.DMA((2, 8)),
             pltpu.SemaphoreType.DMA((2, 8)),
-            pltpu.SemaphoreType.DMA((2,)),
             pltpu.SemaphoreType.REGULAR((3,)),
         ],
         compiler_params=pltpu.CompilerParams(

time: 51.3 us -> 46.8 us (0.912)
  Pallas kernels: 50.5 us -> 46 us
    pallas_call x1, Pallas kernels: 49 us -> 44.4 us  [on_device(): pl.pallas_call(functools.partial(kernel, count, rows_gy), out_shape=(pltp...]
where the time goes in v3:
time: 46.8 us; the launch traced here: 46.7 us
  Pallas kernels  46 us (98%)
  between operations  0.64 us (1%)
    pallas_call x1, Pallas kernels, on_device(): pl.pallas_call(functools.partial(kernel, count, rows_gy), out_shape=(pltp...  44.4 us
    pallas_call x1, Pallas kernels, on_device(): pl.pallas_call(hand_over, out_shape=(jax.ShapeDtypeStruct((9, NX, NY, NZ)...  1.59 us

profile of v3, /device:TPU:34, one launch (start us, length us, event | category | flops | bytes accessed | tf_op | source)
XLA Modules:
  0.0 46.7 jit_solution(952373147164180421)
XLA Ops:
  0.6 44.4 %shard_map.86 = (f32[9,4,32,512]{3,2,1,0:T(8,128)S(1)}, f32[2,4,32,512]{3,2,1,0:T(8,128)S(1)}) custom-call(f32[9,4,32,512]{3,2,1,0:T(8,128)} %adjoint.1, f32[4,32,512]{2,1,0:T(8,128)} %buoyancy.1, f32[4,32,512]{2,1,0:T(8,128)} %lame.1, f32[4,32,512]{2,1,0:T(8,128)} %shear.1, s32[64,24,128]{2,1,0:T(8,128)} %bitcast.4, f32[12,1,64]{2,1,0:T(1,128)} %bitcast.5, ...), custom_call_target="tpu_custom_call" | custom-call | tf_op jit(solution)/shard_map/pallas_call | solution.py:457
  45.1 1.6 %shard_map.87 = (f32[9,4,32,512]{3,2,1,0:T(8,128)}, f32[2,4,32,512]{3,2,1,0:T(8,128)}) custom-call(f32[9,4,32,512]{3,2,1,0:T(8,128)S(1)} %get-tuple-element.4.state, f32[2,4,32,512]{3,2,1,0:T(8,128)S(1)} %get-tuple-element.5.grad), custom_call_target="tpu_custom_call" | custom-call | tf_op jit(solution)/shard_map/pallas_call | solution.py:500

commit v4 on v3

--- a/solution.py
+++ b/solution.py
@@ -13,6 +13,7 @@
 NX, NY, NZ = 4, 32, 512
 TOP, END = 8, 40
 LAST = NX
+RELAYED = 2
 SCALE_UNIT = 2.0**31
 
 
@@ -44,11 +45,11 @@
     count, rows_gy,
     adjoint, buoyancy, lame, shear, words, factors, order,
     out, gradients,
-    field, mat_b, mat_l, mat_m, strain, stored, held, landed,
+    field, mat_b, mat_l, mat_m, strain, stored, held, landed, relay,
     to_lo, to_hi, to_south, to_north, to_corner,
     from_lo, from_hi, from_south, from_north, from_corner,
     square, factor_rows, order_row, inverse_row, inverse,
-    load_sem, send_sem, recv_sem, halo_send, halo_recv, ready,
+    load_sem, send_sem, recv_sem, halo_send, halo_recv, relay_send, relay_recv, ready,
 ):
     me, row = lax.axis_index("gx"), lax.axis_index("gy")
     own_x, own_y = pl.ds(1, NX), pl.ds(TOP, NY)
@@ -90,10 +91,17 @@
     along_x = [peer(d, 0, 0, 0) for d in (1, 2, 3)]
     along_y = [peer(0, 0, d, 0) for d in (1, 2, 3)]
     across_z, across_core = peer(0, 1, 0, 0), peer(0, 0, 0, 1)
-    lines = [across_z] + along_x + along_y + [across_core]
+    other_half = [peer(dx, 1, dy, dcore) for dcore in range(2) for dx in range(4) for dy in range(4)]
+    lines = along_x + along_y + [across_core]
     for other in lines:
         signal(barrier, {"gx": other})
-    expected = jnp.int32(len(lines))
+
+    @pl.when(z == 0)
+    def _():
+        for other in other_half:
+            signal(barrier, {"gx": other})
+
+    expected = len(lines) + len(other_half) * z
     for (dx, dy), there in exists.items():
         expected = expected + there.astype(jnp.int32)
 
@@ -332,15 +340,51 @@
     def exchange(other):
         return pltpu.make_async_remote_copy(
             src_ref=held.at[other, pl.ds(0, 25)], dst_ref=landed.at[me, pl.ds(0, 25)],
-            send_sem=send_sem.at[other], recv_sem=recv_sem.at[me],
+            send_sem=send_sem, recv_sem=recv_sem,
             device_id={"gx": other}, device_id_type=MESH,
         )
 
-    def send_plane(dz, dcore):
+    def blocks_of(ref, sem, number):
+        some = ref.at[pl.ds(0, number), pl.ds(0, 25)]
+        return pltpu.make_async_copy(some, some, sem)
+
+    def send_near(dcore):
         for dx in range(4):
             for dy in range(4):
-                if (dx, dz, dy, dcore) != (0, 0, 0, 0):
-                    exchange(peer(dx, dz, dy, dcore)).start()
+                if (dx, dy, dcore) != (0, 0, 0):
+                    exchange(peer(dx, 0, dy, dcore)).start()
+
+    edge = (y == 0) | (y == 3)
+
+    def send_far(dcore):
+        for dx in range(4):
+            if dx == RELAYED:
+                continue
+            for dy in range(4):
+                exchange(peer(dx, 1, dy, dcore)).start()
+
+    def send_far_middle(dcore):
+        for dy in range(4):
+            exchange(peer(RELAYED, 1, dy, dcore)).start()
+
+    def relayed_owner(n):
+        return at_x[RELAYED] + at_z[1] + n
+
+    def to_relay(n):
+        owner = relayed_owner(n)
+        return pltpu.make_async_remote_copy(
+            src_ref=held.at[owner, pl.ds(0, 25)], dst_ref=relay.at[n, pl.ds(0, 25)],
+            send_sem=send_sem, recv_sem=relay_recv,
+            device_id={"gx": at_x[0] + at_z[0] + (1 + y // 3) * 2 + core}, device_id_type=MESH,
+        )
+
+    def from_relay(n):
+        holder = at_x[0] + at_z[0] + (y - 1) * 3 * 2 + core
+        return pltpu.make_async_remote_copy(
+            src_ref=relay.at[n, pl.ds(0, 25)], dst_ref=landed.at[holder, pl.ds(0, 25)],
+            send_sem=relay_send, recv_sem=recv_sem,
+            device_id={"gx": relayed_owner(n)}, device_id_type=MESH,
+        )
 
     pl.semaphore_wait(barrier, expected)
     send_halo(0, slice(None))
@@ -350,30 +394,60 @@
     loads[6].wait()
     square[16:17, 0:64] = order_row[...].astype(jnp.float32)
     prepare_blocks()
+
+    @pl.when(edge)
+    def _():
+        for n in range(8):
+            to_relay(n).start()
+
+    @pl.when((z == 1) & jnp.logical_not(edge))
+    def _():
+        for dcore in range(2):
+            send_far(dcore)
+            send_far_middle(dcore)
+
     landed[me] = held[me]
     to_smem = pltpu.make_async_copy(inverse_row, inverse, load_sem.at[7])
     to_smem.start()
     pl.semaphore_wait(ready.at[0], 3)
-    signal(ready.at[1], {"gx": across_z})
     signal(ready.at[1], {"gx": across_core})
-    send_plane(0, 0)
-    pl.semaphore_wait(ready.at[1], 2)
-    signal(ready.at[2], {"gx": across_core})
-    send_plane(1, 0)
-    send_plane(0, 1)
-    pl.semaphore_wait(ready.at[2], 1)
-    send_plane(1, 1)
+
+    @pl.when(z == 1)
+    def _():
+        signal(ready.at[2], {"gx": across_z})
+
+    pl.semaphore_wait(ready.at[1], 1)
+
+    @pl.when((z == 1) & edge)
+    def _():
+        send_far(0)
+
+    @pl.when(z == 0)
+    def _():
+        pl.semaphore_wait(ready.at[2], 1)
+        signal(ready.at[3], {"gx": across_core})
+        send_far(0)
+        pl.semaphore_wait(ready.at[3], 1)
+
+    @pl.when((z == 0) & jnp.logical_not(edge))
+    def _():
+        send_far(1)
+
+    @pl.when((z == 0) & jnp.logical_not(edge))
+    def _():
+        send_far_middle(0)
+        send_far_middle(1)
+
+    @pl.when(jnp.logical_not(edge))
+    def _():
+        blocks_of(relay, relay_recv, 8).wait()
+        for n in range(8):
+            from_relay(n).start()
+
+    send_near(0)
+    send_near(1)
     loads[4].wait()
     loads[5].wait()
-
-    def arrive(t, _):
-        other = lax.rem(me + t, count)
-        pltpu.make_async_remote_copy(
-            src_ref=held.at[other, pl.ds(0, 25)], dst_ref=landed.at[other, pl.ds(0, 25)],
-            send_sem=send_sem.at[other], recv_sem=recv_sem.at[other],
-            device_id={"gx": other}, device_id_type=MESH,
-        ).wait()
-        return 0
 
     def correlate(n, _):
         i, k = n // (NY // 8), n % (NY // 8)
@@ -411,22 +485,27 @@
         return 0
 
     tiles = NX * NY // 8
-    lax.fori_loop(0, tiles, move_velocity, 0)
+    lax.fori_loop(0, tiles, move_velocity, 0, unroll=2)
     take_halo(0)
+
+    @pl.when(edge)
+    def _():
+        send_far(1)
+
     finish_halo(0)
-    lax.fori_loop(0, tiles // 2, functools.partial(move_stress, 0, 0, NX - 1), 0)
+    lax.fori_loop(0, tiles // 2, functools.partial(move_stress, 0, 0, NX - 1), 0, unroll=2)
     stage_layers(1)
     send_halo(1, slice(0, 2))
-    lax.fori_loop(0, tiles // 2, functools.partial(move_stress, 0, 1, 1), 0)
+    lax.fori_loop(0, tiles // 2, functools.partial(move_stress, 0, 1, 1), 0, unroll=2)
     stage_rows(1)
     send_halo(1, slice(2, None))
-    lax.fori_loop(0, tiles, move_velocity, 0)
-    lax.fori_loop(1, count, arrive, 0)
+    lax.fori_loop(0, tiles, move_velocity, 0, unroll=2)
+    blocks_of(landed, recv_sem, count - 1).wait()
     to_smem.wait()
-    lax.fori_loop(0, tiles, correlate, 0)
+    lax.fori_loop(0, tiles, correlate, 0, unroll=2)
     take_halo(1)
     finish_halo(1)
-    lax.fori_loop(0, tiles, functools.partial(move_stress, 1, 0, 1), 0)
+    lax.fori_loop(0, tiles, functools.partial(move_stress, 1, 0, 1), 0, unroll=2)
     for step in range(2):
         for copy, there, _ in halo_copies(step):
 
@@ -434,12 +513,16 @@
             def _():
                 copy.wait_send()
 
+    @pl.when(jnp.logical_not(edge))
+    def _():
+        blocks_of(relay, relay_send, 8).wait()
+
+    blocks_of(held, send_sem, count - 1).wait()
+
 
 def hand_over(state, grad, out, gradients, sem):
-    copies = [
-        pltpu.make_async_copy(state, out, sem.at[0]),
-        pltpu.make_async_copy(grad, gradients, sem.at[1]),
-    ]
+    copies = [pltpu.make_async_copy(state.at[f], out.at[f], sem.at[f]) for f in range(9)]
+    copies += [pltpu.make_async_copy(grad.at[f], gradients.at[f], sem.at[9 + f]) for f in range(2)]
     for copy in copies:
         copy.start()
     for copy in copies:
@@ -471,6 +554,7 @@
             pltpu.VMEM((6, NX, NY, NZ), f32),
             pltpu.VMEM((64, 32, 128), i32),
             pltpu.VMEM((64, 32, 128), i32),
+            pltpu.VMEM((8, 32, 128), i32),
             pltpu.VMEM((2, 4, NY, NZ), f32),
             pltpu.VMEM((2, 4, NY, NZ), f32),
             pltpu.VMEM((2, 16, NZ), f32),
@@ -487,11 +571,13 @@
             pltpu.VMEM((1, 128), i32),
             pltpu.SMEM((1, 128), i32),
             pltpu.SemaphoreType.DMA((8,)),
-            pltpu.SemaphoreType.DMA((64,)),
-            pltpu.SemaphoreType.DMA((64,)),
+            pltpu.SemaphoreType.DMA,
+            pltpu.SemaphoreType.DMA,
             pltpu.SemaphoreType.DMA((2, 8)),
             pltpu.SemaphoreType.DMA((2, 8)),
-            pltpu.SemaphoreType.REGULAR((3,)),
+            pltpu.SemaphoreType.DMA,
+            pltpu.SemaphoreType.DMA,
+            pltpu.SemaphoreType.REGULAR((4,)),
         ],
         compiler_params=pltpu.CompilerParams(
             collective_id=0, has_side_effects=True, vmem_limit_bytes=32 * 2**20
@@ -505,7 +591,7 @@
         ),
         in_specs=[any_space] * 2,
         out_specs=(any_space, any_space),
-        scratch_shapes=[pltpu.SemaphoreType.DMA((2,))],
+        scratch_shapes=[pltpu.SemaphoreType.DMA((11,))],
     )(*(pltpu.with_memory_space_constraint(x, pltpu.VMEM) for x in (state, grad)))
 
 

time: 46.8 us -> 43.6 us (0.932)
  Pallas kernels: 46 us -> 42.7 us
    pallas_call x1, Pallas kernels: 44.4 us -> 41.1 us  [on_device(): pl.pallas_call(functools.partial(kernel, count, rows_gy), out_shape=(pltp...]
where the time goes in v4:
time: 43.6 us; the launch traced here: 43.4 us
  Pallas kernels  42.7 us (98%)
  between operations  0.64 us (1%)
    pallas_call x1, Pallas kernels, on_device(): pl.pallas_call(functools.partial(kernel, count, rows_gy), out_shape=(pltp...  41.1 us
    pallas_call x1, Pallas kernels, on_device(): pl.pallas_call(hand_over, out_shape=(jax.ShapeDtypeStruct((9, NX, NY, NZ)...  1.66 us

profile of v4, /device:TPU:34, one launch (start us, length us, event | category | flops | bytes accessed | tf_op | source)
XLA Modules:
  0.0 43.4 jit_solution(14072020948460083427)
XLA Ops:
  0.6 41.1 %shard_map.86 = (f32[9,4,32,512]{3,2,1,0:T(8,128)S(1)}, f32[2,4,32,512]{3,2,1,0:T(8,128)S(1)}) custom-call(f32[9,4,32,512]{3,2,1,0:T(8,128)} %adjoint.1, f32[4,32,512]{2,1,0:T(8,128)} %buoyancy.1, f32[4,32,512]{2,1,0:T(8,128)} %lame.1, f32[4,32,512]{2,1,0:T(8,128)} %shear.1, s32[64,24,128]{2,1,0:T(8,128)} %bitcast.4, f32[12,1,64]{2,1,0:T(1,128)} %bitcast.5, ...), custom_call_target="tpu_custom_call" | custom-call | tf_op jit(solution)/shard_map/pallas_call | solution.py:540
  41.7 1.7 %shard_map.87 = (f32[9,4,32,512]{3,2,1,0:T(8,128)}, f32[2,4,32,512]{3,2,1,0:T(8,128)}) custom-call(f32[9,4,32,512]{3,2,1,0:T(8,128)S(1)} %get-tuple-element.4.state, f32[2,4,32,512]{3,2,1,0:T(8,128)S(1)} %get-tuple-element.5.grad), custom_call_target="tpu_custom_call" | custom-call | tf_op jit(solution)/shard_map/pallas_call | solution.py:586

commit v5 on v4

--- a/solution.py
+++ b/solution.py
@@ -41,11 +41,47 @@
     return pltpu.roll(jnp.where(rows_of(x.shape) == 7, preceding, x), 1, 0)
 
 
+def stress_mover(field, mat_l, mat_m, strain, stored, partial, out=None, gradients=None):
+    def dyn(f, layer, start):
+        return field[f, layer, pl.ds(start, 8), :]
+
+    def move_stress(step, first_layer, stride, n, _):
+        i, k = first_layer + stride * (n // (NY // 8)), n % (NY // 8)
+        layer, at = i + 1, pl.multiple_of(TOP + 8 * k, 8)
+        before, after = pl.multiple_of(8 * k, 8), pl.multiple_of(TOP + 8 + 8 * k, 8)
+        flat = pl.ds(pl.multiple_of(8 * k, 8), 8)
+        vx, vy, vz = (dyn(f, layer, at) for f in (VX, VY, VZ))
+        exx = vx - dyn(VX, layer - 1, at)
+        eyy = vy - y_behind(vy, dyn(VY, layer, before))
+        ezz = vz - z_behind(vz)
+        exy = y_ahead(vx, dyn(VX, layer, after)) - vx + dyn(VY, layer + 1, at) - vy
+        exz = z_ahead(vx) - vx + dyn(VZ, layer + 1, at) - vz
+        eyz = z_ahead(vy) - vy + y_ahead(vz, dyn(VZ, layer, after)) - vz
+        mu = COURANT * mat_m[i, flat, :]
+        both = (COURANT * mat_l[i, flat, :]) * (exx + eyy + ezz)
+        moved = [dyn(f, layer, at) - (both + 2.0 * mu * e) for f, e in ((SXX, exx), (SYY, eyy), (SZZ, ezz))]
+        moved += [dyn(f, layer, at) - mu * e for f, e in ((SXY, exy), (SXZ, exz), (SYZ, eyz))]
+        e = (exx, eyy, ezz, exy, exz, eyz)
+        if step == 0:
+            for f in range(6):
+                field[SXX + f, layer, pl.ds(at, 8), :] = moved[f]
+                strain[f, i, flat, :] = e[f]
+            return 0
+        for f, value in enumerate([vx, vy, vz] + moved):
+            out[f, i, flat, :] = value
+        f = [stored[c, i, flat, :] for c in range(6)]
+        gradients[0, i, flat, :] = partial[0, i, flat, :] + (exx + eyy + ezz) * (f[0] + f[1] + f[2])
+        gradients[1, i, flat, :] = partial[1, i, flat, :] + 2.0 * (exx * f[0] + eyy * f[1] + ezz * f[2]) + exy * f[3] + exz * f[4] + eyz * f[5]
+        return 0
+
+    return move_stress
+
+
 def kernel(
     count, rows_gy,
     adjoint, buoyancy, lame, shear, words, factors, order,
-    out, gradients,
-    field, mat_b, mat_l, mat_m, strain, stored, held, landed, relay,
+    field, mat_l, mat_m, stored, gradients,
+    mat_b, strain, held, landed, relay,
     to_lo, to_hi, to_south, to_north, to_corner,
     from_lo, from_hi, from_south, from_north, from_corner,
     square, factor_rows, order_row, inverse_row, inverse,
@@ -281,34 +317,7 @@
         field[VZ, layer, pl.ds(at, 8), :] = dyn(VZ, layer, at) - b * dz
         return 0
 
-    def move_stress(step, first_layer, stride, n, _):
-        i, k = first_layer + stride * (n // (NY // 8)), n % (NY // 8)
-        layer, at = i + 1, pl.multiple_of(TOP + 8 * k, 8)
-        before, after = pl.multiple_of(8 * k, 8), pl.multiple_of(TOP + 8 + 8 * k, 8)
-        flat = pl.ds(pl.multiple_of(8 * k, 8), 8)
-        vx, vy, vz = (dyn(f, layer, at) for f in (VX, VY, VZ))
-        exx = vx - dyn(VX, layer - 1, at)
-        eyy = vy - y_behind(vy, dyn(VY, layer, before))
-        ezz = vz - z_behind(vz)
-        exy = y_ahead(vx, dyn(VX, layer, after)) - vx + dyn(VY, layer + 1, at) - vy
-        exz = z_ahead(vx) - vx + dyn(VZ, layer + 1, at) - vz
-        eyz = z_ahead(vy) - vy + y_ahead(vz, dyn(VZ, layer, after)) - vz
-        mu = COURANT * mat_m[i, flat, :]
-        both = (COURANT * mat_l[i, flat, :]) * (exx + eyy + ezz)
-        moved = [dyn(f, layer, at) - (both + 2.0 * mu * e) for f, e in ((SXX, exx), (SYY, eyy), (SZZ, ezz))]
-        moved += [dyn(f, layer, at) - mu * e for f, e in ((SXY, exy), (SXZ, exz), (SYZ, eyz))]
-        e = (exx, eyy, ezz, exy, exz, eyz)
-        if step == 0:
-            for f in range(6):
-                field[SXX + f, layer, pl.ds(at, 8), :] = moved[f]
-                strain[f, i, flat, :] = e[f]
-            return 0
-        for f, value in enumerate([vx, vy, vz] + moved):
-            out[f, i, flat, :] = value
-        f = [stored[c, i, flat, :] for c in range(6)]
-        gradients[0, i, flat, :] += (exx + eyy + ezz) * (f[0] + f[1] + f[2])
-        gradients[1, i, flat, :] += 2.0 * (exx * f[0] + eyy * f[1] + ezz * f[2]) + exy * f[3] + exz * f[4] + eyz * f[5]
-        return 0
+    move_stress = stress_mover(field, mat_l, mat_m, strain, stored, gradients)
 
     blank = jnp.zeros((NY, NZ), jnp.float32)
     field[SXX, LAST + 1, pl.ds(TOP, NY), :] = blank
@@ -505,7 +514,6 @@
     lax.fori_loop(0, tiles, correlate, 0, unroll=2)
     take_halo(1)
     finish_halo(1)
-    lax.fori_loop(0, tiles, functools.partial(move_stress, 1, 0, 1), 0, unroll=2)
     for step in range(2):
         for copy, there, _ in halo_copies(step):
 
@@ -520,11 +528,15 @@
     blocks_of(held, send_sem, count - 1).wait()
 
 
-def hand_over(state, grad, out, gradients, sem):
-    copies = [pltpu.make_async_copy(state.at[f], out.at[f], sem.at[f]) for f in range(9)]
-    copies += [pltpu.make_async_copy(grad.at[f], gradients.at[f], sem.at[9 + f]) for f in range(2)]
-    for copy in copies:
-        copy.start()
+def last_step(field, mat_l, mat_m, stored, partial, out, gradients, state, grad, sem):
+    move_stress = stress_mover(field, mat_l, mat_m, None, stored, partial, state, grad)
+    copies = []
+    for i in range(NX):
+        lax.fori_loop(0, NY // 8, functools.partial(move_stress, 1, i, 1), 0, unroll=2)
+        copies.append(pltpu.make_async_copy(state.at[:, i], out.at[:, i], sem.at[2 * i]))
+        copies.append(pltpu.make_async_copy(grad.at[:, i], gradients.at[:, i], sem.at[2 * i + 1]))
+        copies[-2].start()
+        copies[-1].start()
     for copy in copies:
         copy.wait()
 
@@ -537,20 +549,19 @@
     f32, i32 = jnp.float32, jnp.int32
     inputs = (adjoint, buoyancy, lame_lambda, shear_mu, words, factors, perm)
     inputs = [pltpu.with_memory_space_constraint(x, pltpu.HBM) for x in inputs]
-    state, grad = pl.pallas_call(
+    handed = pl.pallas_call(
         functools.partial(kernel, count, rows_gy),
         out_shape=(
-            pltpu.VMEM((9, NX, NY, NZ), f32),
+            pltpu.VMEM((9, NX + 2, NY + 16, NZ), f32),
+            pltpu.VMEM((NX, NY, NZ), f32),
+            pltpu.VMEM((NX, NY, NZ), f32),
+            pltpu.VMEM((6, NX, NY, NZ), f32),
             pltpu.VMEM((2, NX, NY, NZ), f32),
         ),
         in_specs=[any_space] * 7,
-        out_specs=(in_vmem, in_vmem),
+        out_specs=(in_vmem,) * 5,
         scratch_shapes=[
-            pltpu.VMEM((9, NX + 2, NY + 16, NZ), f32),
             pltpu.VMEM((NX, NY, NZ), f32),
-            pltpu.VMEM((NX, NY, NZ), f32),
-            pltpu.VMEM((NX, NY, NZ), f32),
-            pltpu.VMEM((6, NX, NY, NZ), f32),
             pltpu.VMEM((6, NX, NY, NZ), f32),
             pltpu.VMEM((64, 32, 128), i32),
             pltpu.VMEM((64, 32, 128), i32),
@@ -584,15 +595,20 @@
         ),
     )(*inputs)
     return pl.pallas_call(
-        hand_over,
+        last_step,
         out_shape=(
             jax.ShapeDtypeStruct((9, NX, NY, NZ), f32),
             jax.ShapeDtypeStruct((2, NX, NY, NZ), f32),
         ),
-        in_specs=[any_space] * 2,
+        in_specs=[in_vmem] * 5,
         out_specs=(any_space, any_space),
-        scratch_shapes=[pltpu.SemaphoreType.DMA((11,))],
-    )(*(pltpu.with_memory_space_constraint(x, pltpu.VMEM) for x in (state, grad)))
+        scratch_shapes=[
+            pltpu.VMEM((9, NX, NY, NZ), f32),
+            pltpu.VMEM((2, NX, NY, NZ), f32),
+            pltpu.SemaphoreType.DMA((2 * NX,)),
+        ],
+        compiler_params=pltpu.CompilerParams(vmem_limit_bytes=8 * 2**20),
+    )(*(pltpu.with_memory_space_constraint(x, pltpu.VMEM) for x in handed))
 
 
 def solution(mesh):

time: 43.6 us -> 42.9 us (0.984)
  Pallas kernels: 42.7 us -> 42 us
    pallas_call x1, Pallas kernels: 41.1 us -> 40.1 us  [on_device(): pl.pallas_call(functools.partial(kernel, count, rows_gy), out_shape=(pltp...]
where the time goes in v5:
time: 42.9 us; the launch traced here: 42.7 us
  Pallas kernels  42 us (98%)
  between operations  0.64 us (1%)
    pallas_call x1, Pallas kernels, on_device(): pl.pallas_call(functools.partial(kernel, count, rows_gy), out_shape=(pltp...  40.1 us
    pallas_call x1, Pallas kernels, on_device(): pl.pallas_call(last_step, out_shape=(jax.ShapeDtypeStruct((9, NX, NY, NZ)...  1.95 us

profile of v5, /device:TPU:34, one launch (start us, length us, event | category | flops | bytes accessed | tf_op | source)
XLA Modules:
  0.0 42.7 jit_solution(7173336732429644988)
XLA Ops:
  0.6 40.1 %shard_map.86 = (f32[9,6,48,512]{3,2,1,0:T(8,128)S(1)}, f32[4,32,512]{2,1,0:T(8,128)S(1)}, f32[4,32,512]{2,1,0:T(8,128)S(1)}, f32[6,4,32,512]{3,2,1,0:T(8,128)S(1)}, f32[2,4,32,512]{3,2,1,0:T(8,128)S(1)}) custom-call(f32[9,4,32,512]{3,2,1,0:T(8,128)} %adjoint.1, f32[4,32,512]{2,1,0:T(8,128)} %buoyancy.1, f32[4,32,512]{2,1,0:T(8,128)} %lame.1, ...), custom_call_target="tpu_custom_call" | custom-call | tf_op jit(solution)/shard_map/pallas_call | solution.py:552
  40.7 1.9 %shard_map.87 = (f32[9,4,32,512]{3,2,1,0:T(8,128)}, f32[2,4,32,512]{3,2,1,0:T(8,128)}) custom-call(f32[9,6,48,512]{3,2,1,0:T(8,128)S(1)} %get-tuple-element.7.field, f32[4,32,512]{2,1,0:T(8,128)S(1)} %get-tuple-element.8.mat_l, f32[4,32,512]{2,1,0:T(8,128)S(1)} %get-tuple-element.9.mat_m, f32[6,4,32,512]{3,2,1,0:T(8,128)S(1)} %get-tuple-element.10.stored, ...), custom_call_target="tpu_custom_call" | custom-call | tf_op jit(solution)/shard_map/pallas_call | solution.py:597
